TPU v7x, 1024 devices: a whole 8x8x8 slice. The times are simulated.
1024 devices in a mesh: row: 64 (over y, x), col: 16 (over z, core).
Axes of the slice: x: 8, y: 8, z: 8, core: 2. Of those that a mesh axis runs over, the one named last changes fastest.
Arguments:
- points: bfloat16 [16, 16384, 768], P('col', 'row'), may hold values from -6 to 6
- candidates: int32 [16, 2048, 4], P('col', 'row'), may hold values from 0 to 63, all different within a row; in each aligned block of 32 rows (0 to 31, 32 to 63, ..., all dimensions but the last counted through in order) at most 4 rows name the same one
- centroids: float32 [64, 256, 768], P('row'), may hold values from -2 to 2
- prices: float32 [64, 256], P('row'), may hold values from -1 to 1
Outputs:
- new_centroids: float32 [64, 256, 768], P('row')
- new_prices: float32 [64, 256], P('row')
Inputs may be any that keep to these rules, and one draw needn't show every extreme that they name: `candidates`: each block names 4 different cells. Among the 32 blocks of one device no cell is named by more than 4 blocks, and in every draw some device has a cell named by exactly 4 of its blocks.
All inputs are finite; a program needn't handle non-finite values.
Results may differ from a plain program's by a relative error of at most 0.0065.
The roundings to bfloat16 on the way count: a program that leaves them out, or rounds other values in their place, can miss the bound.
Values may be sent and summed in bfloat16 or wider, within the bound.
No kernel may reach another device: no remote copies, remote signals or barrier semaphores. Data moves between devices by JAX's collectives and lax.ppermute only.
A program may use at most 64 MiB of HBM per device.

v0:
```python
import jax
import jax.numpy as jnp
from jax import lax
from jax.sharding import PartitionSpec as P

STEPS = 2


prior_mass = 1.0
price_rate = 0.5


def sent_together(arrays, axis, split_dim, concat_dim, along):
    columns = [a.reshape(*a.shape[:along], -1) for a in arrays]
    both = jnp.concatenate(columns, axis=along)
    filled, at, done = (
        lax.all_to_all(both, axis, split_axis=split_dim, concat_axis=concat_dim, tiled=True),
        0,
        [],
    )
    for a, column in zip(arrays, columns):
        piece = filled[..., at : at + column.shape[along]]
        done.append(piece.reshape(*piece.shape[:along], *a.shape[along:]))
        at += column.shape[along]
    return tuple(done)


def side_by_side(arrays, axis, split_dim, concat_dim, along):
    widths = [a.shape[along] for a in arrays]
    both = jnp.concatenate(arrays, axis=along)
    filled = lax.all_to_all(both, axis, split_axis=split_dim, concat_axis=concat_dim, tiled=True)
    return tuple(jnp.split(filled, [sum(widths[:k]) for k in range(1, len(widths))], axis=along))


def over_pieces(shard, axis):
    blocks = lax.all_gather(shard, axis)
    return blocks.sum(axis=0)


def shards(points, candidates, centroids, prices):
    row_count = lax.axis_size("row")
    col_count = lax.axis_size("col")
    wanted = candidates[0]
    block_count, top_count = wanted.shape
    width = points.shape[2]
    centres = centroids.shape[1]
    per_block = points.shape[1] // block_count
    capacity = max(2, (2 * top_count * block_count + row_count - 1) // row_count)
    owners = jnp.arange(row_count, dtype=jnp.int32)
    named = jnp.sum((wanted[:, :, None] == owners[None, None, :]).astype(jnp.float32), axis=1)
    before = jnp.cumsum(named, axis=0) - named
    slot_ids = jnp.arange(capacity, dtype=jnp.float32)
    slot_map = named.T[:, None, :] * (before.T[:, None, :] == slot_ids[None, :, None]).astype(
        jnp.float32
    )
    flat_map = slot_map.reshape(row_count * capacity, block_count)
    blocks = points[0].reshape(block_count, per_block * width)
    outgoing = jnp.dot(flat_map.astype(jnp.bfloat16), blocks, preferred_element_type=jnp.float32)
    outgoing = outgoing.astype(jnp.bfloat16).reshape(row_count, capacity, per_block, width)
    occupied = jnp.sum(slot_map, axis=-1).astype(jnp.bfloat16)
    arrived, arrived_mask = sent_together((outgoing, occupied), "row", 0, 0, 2)
    incoming = arrived.reshape(row_count * capacity * per_block, width)
    row_mask = jnp.repeat(arrived_mask.astype(jnp.float32).reshape(-1), per_block)
    target = col_count * block_count * per_block / centres
    means = centroids[0]
    price = prices[0]
    for sweep_index in range(STEPS):
        offset = 0.5 * jnp.sum(means * means, axis=-1) + price
        scores = (
            lax.dot_general(
                incoming,
                means.astype(jnp.bfloat16),
                (((1,), (1,)), ((), ())),
                preferred_element_type=jnp.float32,
            )
            - offset[None, :]
        )
        highest = jnp.max(scores, axis=-1)
        masses = jnp.sum(jnp.exp(scores - highest[:, None]), axis=-1)
        shape_back = (row_count, capacity, per_block)
        top_back, mass_back = side_by_side(
            (highest.reshape(shape_back), masses.reshape(shape_back)), "row", 0, 0, 1
        )
        block_top = jnp.einsum("osb,osp->bop", slot_map, top_back, precision=lax.Precision.HIGHEST)
        block_mass = jnp.einsum(
            "osb,osp->bop", slot_map, mass_back, precision=lax.Precision.HIGHEST
        )
        masked = jnp.where(named[:, :, None] > 0, block_top, jnp.float32(-1e30))
        largest = jnp.max(masked, axis=1)
        totals = jnp.sum(
            named[:, :, None] * block_mass * jnp.exp(masked - largest[:, None, :]), axis=1
        )
        norm_log = largest + jnp.log(totals)
        slot_log = jnp.einsum("osb,bp->osp", slot_map, norm_log, precision=lax.Precision.HIGHEST)
        arrived_log = lax.all_to_all(slot_log, "row", split_axis=0, concat_axis=0, tiled=True)
        weight = jnp.exp(scores - arrived_log.reshape(-1)[:, None]) * row_mask[:, None]
        load_sums = jnp.sum(weight, axis=0)
        point_sums = lax.dot_general(
            weight.astype(jnp.bfloat16),
            incoming,
            (((0,), (0,)), ((), ())),
            preferred_element_type=jnp.float32,
        )
        point_sums, load_sums = (point_sums, load_sums)
        point_sums, load_sums = (over_pieces(point_sums, "col"), over_pieces(load_sums, "col"))
        new_means = (point_sums + prior_mass * means) / (load_sums[:, None] + prior_mass)
        price = price + price_rate * jnp.log((load_sums + prior_mass) / (target + prior_mass))
        means = new_means
    return (means[None], price[None])


def solution(mesh):
    placed = (P("col", "row", None), P("col", "row", None), P("row", None, None), P("row", None))
    return jax.shard_map(
        shards,
        mesh=mesh,
        in_specs=placed,
        out_specs=(P("row", None, None), P("row", None)),
        check_vma=False,
    )
```

profile of v0, /device:TPU:1, one launch (start us, length us, event | category | flops | bytes accessed | tf_op | source)
XLA Modules:
  0.0 428.7 jit_solution(10106186055993872652)
XLA Ops:
  11.6 1.8 convolution_convert_fusion
  13.4 2.7 reshape_reshape.6
  16.1 5.2 %pad_maximum_fusion = bf16[64,4,6145]{2,1,0:T(4,128)(2,1)} fusion(bf16[64,4,1]{2,1,0:T(4,128)(2,1)S(1)} %copy-done.9, bf16[64,4,6144]{2,1,0:T(4,128)(2,1)} %reshape_reshape.6), kind=kLoop, calls=%fused_computation.1 | loop fusion | flops 6292480 | bytes 6292480 | tf_op jit(solution)/shard_map/concatenate | solution.py:15
  21.2 14.2 %all-to-all-start = ((bf16[64,4,6145]{2,1,0:T(4,128)(2,1)}), bf16[64,4,6145]{2,1,0:T(4,128)(2,1)S(1)}, u32[]{:S(2)}, u32[]{:S(2)}) async-start(bf16[64,4,6145]{2,1,0:T(4,128)(2,1)} %pad_maximum_fusion), calls=%async_computation | async-start | bytes 6422528 | tf_op jit(solution)/shard_map/all_to_all | solution.py:17
  36.7 67.8 %all-to-all-done = bf16[64,4,6145]{2,1,0:T(4,128)(2,1)S(1)} async-done(((bf16[64,4,6145]{2,1,0:T(4,128)(2,1)}), bf16[64,4,6145]{2,1,0:T(4,128)(2,1)S(1)}, u32[]{:S(2)}, u32[]{:S(2)}) %all-to-all-start) | async-done | bytes 3146272 | tf_op jit(solution)/shard_map/all_to_all | solution.py:17
  104.5 3.4 slice.8
  107.9 6.5 %reshape_reshape.7 = bf16[2048,768]{1,0:T(8,128)(2,1)} reshape(bf16[64,4,6144]{2,1,0:T(4,128)(2,1)} %slice.8) | data formatting | bytes 6291456 | tf_op jit(solution)/shard_map/reshape;reshape | solution.py:62
  114.4 4.4 %fusion.65 = (f32[2048]{0:T(1024)S(1)}, f32[2048,256]{0,1:T(8,128)}) fusion(f32[256]{0:T(256)S(1)} %bitcast.103, bf16[2048,768]{1,0:T(8,128)(2,1)} %reshape_reshape.7, f32[1,256,768]{2,1,0:T(8,128)} %param.6), kind=kOutput, calls=%fused_computation.94 | convolution fusion | flops 806549504 | bytes 6038528 | tf_op jit(solution)/shard_map/dot_general | solution.py:70
  119.0 2.5 exponential_reduce_fusion.1
  123.2 14.0 %all-to-all-start.1 = ((f32[64,8,8]{2,1,0:T(8,128)}), f32[64,8,8]{2,1,0:T(8,128)S(1)}, u32[]{:S(2)}, u32[]{:S(2)}) async-start(f32[64,8,8]{2,1,0:T(8,128)} %pad_maximum_fusion.1), calls=%async_computation.1 | async-start | bytes 524288 | tf_op jit(solution)/shard_map/all_to_all | solution.py:31
  140.8 8.8 %all-to-all-done.1 = f32[64,8,8]{2,1,0:T(8,128)S(1)} async-done(((f32[64,8,8]{2,1,0:T(8,128)}), f32[64,8,8]{2,1,0:T(8,128)S(1)}, u32[]{:S(2)}, u32[]{:S(2)}) %all-to-all-start.1) | async-done | bytes 16416 | tf_op jit(solution)/shard_map/all_to_all | solution.py:31
  153.6 4.6 %all-to-all-start.2 = ((f32[64,4,8]{2,1,0:T(4,128)}), f32[64,4,8]{2,1,0:T(4,128)S(1)}, u32[]{:S(2)}, u32[]{:S(2)}) async-start(f32[64,4,8]{2,1,0:T(4,128)} %copy.70), calls=%async_computation.2 | async-start | bytes 262144 | tf_op jit(solution)/shard_map/all_to_all | solution.py:95
  158.9 10.8 %all-to-all-done.2 = f32[64,4,8]{2,1,0:T(4,128)S(1)} async-done(((f32[64,4,8]{2,1,0:T(4,128)}), f32[64,4,8]{2,1,0:T(4,128)S(1)}, u32[]{:S(2)}, u32[]{:S(2)}) %all-to-all-start.2) | async-done | bytes 8224 | tf_op jit(solution)/shard_map/all_to_all | solution.py:95
  169.9 4.6 %fusion.14 = f32[256,768]{1,0:T(8,128)} fusion(bf16[2048,768]{1,0:T(8,128)(2,1)} %reshape_reshape.7, f32[2048,256]{0,1:T(8,128)} %get-tuple-element.11, f32[2048]{0:T(1024)S(1)} %mul.111, f32[2048]{0:T(1024)S(1)} %sub.84), kind=kOutput, calls=%fused_computation.25 | convolution fusion | flops 806879232 | bytes 6045696 | tf_op jit(solution)/shard_map/dot_general | solution.py:98
  175.0 54.4 %all-gather.4 = f32[16,1,256]{2,1,0:T(1,128)S(1)} all-gather(f32[1,1,256]{2,1,0:T(1,128)S(1)} %bitcast.96), channel_id=3, replica_groups=mesh['row'=64,'col'=16] {'col'}, dimensions={0}, use_global_device_ids=true | all-gather | bytes 17408 | tf_op jit(solution)/shard_map/all_gather | solution.py:36
  229.4 54.0 %all-gather.9.cloned.1.call-done = f32[4096,768]{1,0:T(8,128)} async-done(((f32[256,768]{1,0:T(8,128)}), f32[4096,768]{1,0:T(8,128)}) %all-gather.9.cloned.1.call-update) | async-done | bytes 12582928 | tf_op jit(solution)/shard_map/all_gather | solution.py:36
  283.5 5.5 %reduce_sum.138 = f32[256,768]{1,0:T(8,128)S(1)} reduce(f32[16,256,768]{2,1,0:T(8,128)} %bitcast.92, f32[]{:T(128)} %constant.6.clone.1), dimensions={0}, to_apply=%region_8.9 | reduce | flops 2949120 | bytes 13369348 | tf_op jit(solution)/shard_map/reduce_sum | solution.py:37
  289.8 3.1 fusion.67
  293.8 25.5 %all_to_all.25 = f32[64,8,8]{2,1,0:T(8,128)S(1)} all-to-all(f32[64,8,8]{2,1,0:T(8,128)S(1)} %pad_maximum_fusion.2), channel_id=1, replica_groups=mesh['row'=64,'col'=16] {'row'}, dimensions={0} | all-to-all | bytes 32768 | tf_op jit(solution)/shard_map/all_to_all | solution.py:31
  321.0 16.5 %all_to_all.26 = f32[64,4,8]{2,1,0:T(4,128)S(1)} all-to-all(f32[64,4,8]{2,1,0:T(4,128)S(1)} %copy.72), channel_id=1, replica_groups=mesh['row'=64,'col'=16] {'row'}, dimensions={0} | all-to-all | bytes 16384 | tf_op jit(solution)/shard_map/all_to_all | solution.py:95
  337.6 3.8 fusion.12
  341.9 18.1 %all-gather.5 = f32[16,1,256]{2,1,0:T(1,128)S(1)} all-gather(f32[1,1,256]{2,1,0:T(1,128)S(1)} %bitcast.95), channel_id=5, replica_groups=mesh['row'=64,'col'=16] {'col'}, dimensions={0}, use_global_device_ids=true | all-gather | bytes 17408 | tf_op jit(solution)/shard_map/all_gather | solution.py:36
  360.6 54.7 %all-gather.11.cloned.1.call-done = f32[4096,768]{1,0:T(8,128)} async-done(((f32[256,768]{1,0:T(8,128)}), f32[4096,768]{1,0:T(8,128)}) %all-gather.11.cloned.1.call-update) | async-done | bytes 12582928 | tf_op jit(solution)/shard_map/all_gather | solution.py:36
  415.3 5.5 %reduce_sum.145 = f32[256,768]{1,0:T(8,128)S(1)} reduce(f32[16,256,768]{2,1,0:T(8,128)} %bitcast.91, f32[]{:T(128)} %constant.6.clone.1), dimensions={0}, to_apply=%region_16.17 | reduce | flops 2949120 | bytes 13369348 | tf_op jit(solution)/shard_map/reduce_sum | solution.py:37
  (79 shorter events, 22.1 us)
Async XLA Ops:
  8.1 3.5 copy-start.4
  8.2 3.4 copy-start.6
  13.4 2.7 copy-start.9
  21.2 15.4 %copy-start.11 = (f32[1,256]{1,0:T(1,128)S(1)}, f32[1,256]{1,0:T(1,128)}, u32[]{:S(2)}) copy-start(f32[1,256]{1,0:T(1,128)} %param.7) | copy-start | bytes 3076
  21.2 83.3 %all-to-all-start = ((bf16[64,4,6145]{2,1,0:T(4,128)(2,1)}), bf16[64,4,6145]{2,1,0:T(4,128)(2,1)S(1)}, u32[]{:S(2)}, u32[]{:S(2)}) async-start(bf16[64,4,6145]{2,1,0:T(4,128)(2,1)} %pad_maximum_fusion), calls=%async_computation | async-start | bytes 6422528 | tf_op jit(solution)/shard_map/all_to_all | solution.py:17
  118.8 30.9 %copy-start.5 = (f32[64,32]{1,0:T(8,128)S(1)}, f32[64,32]{1,0:T(8,128)}, u32[]{:S(2)}) copy-start(f32[64,32]{1,0:T(8,128)} %copy-done.4) | copy-start | bytes 24580
  118.8 30.9 %copy-start.7 = (f32[64,32]{1,0:T(8,128)S(1)}, f32[64,32]{1,0:T(8,128)}, u32[]{:S(2)}) copy-start(f32[64,32]{1,0:T(8,128)} %copy-done.6) | copy-start | bytes 24580
  123.2 26.5 %all-to-all-start.1 = ((f32[64,8,8]{2,1,0:T(8,128)}), f32[64,8,8]{2,1,0:T(8,128)S(1)}, u32[]{:S(2)}, u32[]{:S(2)}) async-start(f32[64,8,8]{2,1,0:T(8,128)} %pad_maximum_fusion.1), calls=%async_computation.1 | async-start | bytes 524288 | tf_op jit(solution)/shard_map/all_to_all | solution.py:31
  153.6 16.2 %all-to-all-start.2 = ((f32[64,4,8]{2,1,0:T(4,128)}), f32[64,4,8]{2,1,0:T(4,128)S(1)}, u32[]{:S(2)}, u32[]{:S(2)}) async-start(f32[64,4,8]{2,1,0:T(4,128)} %copy.70), calls=%async_computation.2 | async-start | bytes 262144 | tf_op jit(solution)/shard_map/all_to_all | solution.py:95
  158.2 125.3 %all-gather.9.cloned.1.call-start = ((), (), s32[]{:S(2)}) async-start(), calls=%async_computation.5 | async-start | bytes 13369344 | tf_op jit(solution)/shard_map/all_gather | solution.py:36
  169.9 4.6 %copy-start = (f32[2048,256]{0,1:T(8,128)S(1)}, f32[2048,256]{0,1:T(8,128)}, u32[]{:S(2)}) copy-start(f32[2048,256]{0,1:T(8,128)} %get-tuple-element.11) | copy-start | bytes 6291460
  174.5 240.8 %all-gather.11.cloned.1.call-start = ((), (), s32[]{:S(2)}) async-start(), calls=%async_computation.6 | async-start | bytes 13369344 | tf_op jit(solution)/shard_map/all_gather | solution.py:36
  283.5 5.5 %copy-start.1 = (f32[1,256,768]{2,1,0:T(8,128)S(1)}, f32[1,256,768]{2,1,0:T(8,128)}, u32[]{:S(2)}) copy-start(f32[1,256,768]{2,1,0:T(8,128)} %param.6) | copy-start | bytes 2359300
  283.5 5.8 %copy-start.12 = (f32[1,256]{1,0:T(1,128)S(1)}, f32[1,256]{1,0:T(1,128)}, u32[]{:S(2)}) copy-start(f32[1,256]{1,0:T(1,128)} %param.7) | copy-start | bytes 3076
  289.0 0.9 copy-start.2
  293.0 27.0 %copy-start.10 = (f32[32,64]{0,1:T(8,128)S(1)}, f32[32,64]{0,1:T(8,128)}, u32[]{:S(2)}) copy-start(f32[32,64]{0,1:T(8,128)} %copy.68) | copy-start | bytes 24580
  293.2 27.5 %copy-start.8 = (f32[64,4,32]{0,2,1:T(8,128)S(1)}, f32[64,4,32]{0,2,1:T(8,128)}, u32[]{:S(2)}) copy-start(f32[64,4,32]{0,2,1:T(8,128)} %copy.69) | copy-start | bytes 98308
  415.3 5.5 %copy-start.3 = (f32[256,768]{1,0:T(8,128)S(1)}, f32[256,768]{1,0:T(8,128)}, u32[]{:S(2)}) copy-start(f32[256,768]{1,0:T(8,128)} %copy-done.2) | copy-start | bytes 2359300
Sparse Core Ops, SparseCore 0:
  174.6 108.8 all-gather.8
  341.6 73.6 all-gather.10
where the time goes:
time: 430 us; the launch traced here: 429 us
  waiting for transfers between devices  196 us (46%)
  blocking collectives  114 us (27%)
  starting transfers between devices  33 us (8%)
  other arithmetic  26.9 us (6%)
  matrix products  22.4 us (5%)
  local copies, waits for them, and re-layouts  21.4 us (5%)
  between operations  14.3 us (3%)
    all_gather x2, waiting for transfers between devices, over_pieces(): blocks = lax.all_gather(shard, axis)  109 us
    all_gather x2, blocking collectives, over_pieces(): blocks = lax.all_gather(shard, axis)  72.5 us
    all_to_all x1, waiting for transfers between devices, sent_together(): lax.all_to_all(both, axis, split_axis=split_dim, concat_axis=concat_dim,...  67.8 us
    all_to_all x1, blocking collectives, side_by_side(): lax.all_to_all(both, axis, split_axis=split_dim, concat_axis=concat_dim,...  25.5 us
    all_to_all x1, blocking collectives, shards(): lax.all_to_all(slot_log, 'row', split_axis=0, concat_axis=0, tiled=True)  16.5 us
    all_to_all x1, starting transfers between devices, sent_together(): lax.all_to_all(both, axis, split_axis=split_dim, concat_axis=concat_dim,...  14.2 us
    all_to_all x1, starting transfers between devices, side_by_side(): lax.all_to_all(both, axis, split_axis=split_dim, concat_axis=concat_dim,...  14 us
    reduce_sum x4, other arithmetic, over_pieces(): return blocks.sum(axis=0)  11 us
  transfers between devices with their start and end apart: 5, of which 5 were waited for; matrix products, arithmetic and copies ran while one was open for 2% of the time, Pallas kernels for 0%

commit v1 on v0

v1 whole, which is shorter than its diff:
```python
import functools

import jax
import jax.numpy as jnp
from jax import lax
from jax.experimental import pallas as pl
from jax.experimental.pallas import tpu as pltpu
from jax.sharding import PartitionSpec as P

STEPS = 2
LANES = 128

prior_mass = 1.0
price_rate = 0.5
empty_log = 1e30

VMEM = pl.BlockSpec(memory_space=pltpu.VMEM)


def iota(shape, dim):
    return lax.broadcasted_iota(jnp.int32, shape, dim)


def exact_dot(a, b, dims):
    return lax.dot_general(
        a,
        b,
        (dims, ((), ())),
        precision=lax.Precision.HIGHEST,
        preferred_element_type=jnp.float32,
    )


def small_dot(a, b, dims):
    return lax.dot_general(
        a.astype(jnp.bfloat16),
        b.astype(jnp.bfloat16),
        (dims, ((), ())),
        preferred_element_type=jnp.float32,
    )


def block_names(wanted, cells):
    tops, count = wanted.shape
    cell = iota((cells, count), 0)
    hot = [(wanted[t : t + 1, :] == cell).astype(jnp.float32) for t in range(tops)]
    named = functools.reduce(jnp.add, hot)
    earlier = (iota((count, count), 0) < iota((count, count), 1)).astype(jnp.float32)
    before = small_dot(named, earlier, ((1,), (0,)))
    return hot, named, before


def pack_kernel(cells, capacity, per_block, wanted_ref, points_ref, out_ref):
    wanted = wanted_ref[...]
    count = wanted.shape[1]
    rows = count * per_block
    total = cells * capacity * per_block
    _, named, before = block_names(wanted, cells)
    both = jnp.concatenate([named, before], axis=1)
    chunk = total // 4
    for k in range(4):
        place = iota((chunk, 1), 0) + k * chunk
        owner = (place // (capacity * per_block) == iota((chunk, cells), 1)).astype(jnp.float32)
        spread = small_dot(owner, both, ((1,), (0,)))
        slot = ((place // per_block) % capacity).astype(jnp.float32)
        chosen = spread[:, :count] * (spread[:, count:] == slot).astype(jnp.float32)
        block = iota((chunk, count), 1).astype(jnp.float32)
        source = jnp.sum(chosen * (block + 1.0), axis=1, keepdims=True) - 1.0
        source = source.astype(jnp.int32) * per_block + place % per_block
        pick = (iota((chunk, rows), 1) == source).astype(jnp.float32).astype(jnp.bfloat16)
        moved = jnp.dot(pick, points_ref[...], preferred_element_type=jnp.float32)
        out_ref[k * chunk : (k + 1) * chunk, :] = moved.astype(jnp.bfloat16)


def centre_offset(packed, width):
    return (
        packed[:, width : width + 1].astype(jnp.float32)
        + packed[:, width + 1 : width + 2].astype(jnp.float32)
        + packed[:, width + 2 : width + 3].astype(jnp.float32)
    )


def score_chunk(half, offset, rows):
    return (
        lax.dot_general(half, rows, (((1,), (1,)), ((), ())), preferred_element_type=jnp.float32)
        - offset
    )


def stats_kernel(chunks, packed_ref, incoming_ref, out_ref):
    width = incoming_ref.shape[1]
    packed = packed_ref[...]
    half = packed[:, :width]
    offset = centre_offset(packed, width)
    size = incoming_ref.shape[0] // chunks
    per_owner = out_ref.shape[1]
    part = size // per_owner
    own = iota((part, size), 1) // per_owner == iota((part, size), 0)
    fold = (iota((size, per_owner), 0) % per_owner == iota((size, per_owner), 1)).astype(
        jnp.float32
    )
    for k in range(chunks):
        scores = score_chunk(half, offset, incoming_ref[k * size : (k + 1) * size, :])
        highest = jnp.max(scores, axis=0, keepdims=True)
        mass = jnp.sum(jnp.exp(scores - highest), axis=0, keepdims=True)
        logs = jnp.where(own, highest + jnp.log(mass), 0.0)
        out_ref[k * part : (k + 1) * part, :] = exact_dot(logs, fold, ((1,), (0,)))


def norm_kernel(per_block, capacity, wanted_ref, back_ref, out_ref):
    back = back_ref[...]
    cells = back.shape[0]
    hots, _, before = block_names(wanted_ref[...], cells)
    tops = len(hots)
    count = hots[0].shape[1]
    hot = jnp.concatenate(hots, axis=1)
    slot = small_dot(
        hot * jnp.concatenate([before] * tops, axis=1),
        jnp.ones((cells, capacity * per_block), jnp.float32),
        ((0,), (0,)),
    )
    in_slot = slot == (iota(slot.shape, 1) // per_block).astype(jnp.float32)
    found = jnp.where(in_slot, exact_dot(hot, back, ((0,), (0,))), 0.0)
    part = found[:, :per_block]
    for s in range(1, capacity):
        part = part + found[:, s * per_block : (s + 1) * per_block]
    parts = [part[t * count : (t + 1) * count] for t in range(tops)]
    largest = functools.reduce(jnp.maximum, parts)
    total = functools.reduce(jnp.add, [jnp.exp(part - largest) for part in parts])
    norm = largest + jnp.log(total)
    norm = jnp.concatenate([norm] * capacity, axis=1)
    norm = jnp.where(in_slot, jnp.concatenate([norm] * tops, axis=0), 0.0)
    value = exact_dot(hot, norm, ((1,), (0,)))
    filled = small_dot(hot, in_slot.astype(jnp.float32), ((1,), (0,)))
    out_ref[...] = jnp.where(filled > 0, value, empty_log)


def sums_kernel(chunks, packed_ref, incoming_ref, log_ref, out_ref):
    width = incoming_ref.shape[1]
    packed = packed_ref[...]
    half = packed[:, :width]
    offset = centre_offset(packed, width)
    centres = packed.shape[0]
    size = incoming_ref.shape[0] // chunks
    per_owner = log_ref.shape[1]
    part = size // per_owner
    own = iota((part, size), 1) // per_owner == iota((part, size), 0)
    fold = (iota((per_owner, size), 1) % per_owner == iota((per_owner, size), 0)).astype(
        jnp.float32
    )
    total = jnp.zeros((centres, width), jnp.float32)
    load = jnp.zeros((centres, 1), jnp.float32)
    for k in range(chunks):
        rows = incoming_ref[k * size : (k + 1) * size, :]
        logs = exact_dot(log_ref[k * part : (k + 1) * part, :], fold, ((1,), (0,)))
        logs = jnp.sum(jnp.where(own, logs, 0.0), axis=0, keepdims=True)
        weight = jnp.exp(score_chunk(half, offset, rows) - logs)
        load = load + jnp.sum(weight, axis=1, keepdims=True)
        total = total + jnp.dot(
            weight.astype(jnp.bfloat16), rows, preferred_element_type=jnp.float32
        )
    out_ref[...] = packed_with(total, load)


def packed_with(means, column):
    high = column.astype(jnp.bfloat16)
    rest = column - high.astype(jnp.float32)
    middle = rest.astype(jnp.bfloat16)
    low = (rest - middle.astype(jnp.float32)).astype(jnp.bfloat16)
    lane = iota((means.shape[0], LANES), 1)
    zero = jnp.zeros((means.shape[0], LANES), jnp.bfloat16).astype(jnp.float32)
    tail = jnp.where(
        lane == 0,
        high.astype(jnp.float32),
        jnp.where(
            lane == 1,
            middle.astype(jnp.float32),
            jnp.where(lane == 2, low.astype(jnp.float32), zero),
        ),
    )
    return jnp.concatenate([means.astype(jnp.bfloat16), tail.astype(jnp.bfloat16)], axis=1)


def start_kernel(means_ref, price_ref, out_ref):
    means = means_ref[...]
    offset = 0.5 * jnp.sum(means * means, axis=1, keepdims=True) + price_ref[...]
    out_ref[...] = packed_with(means, offset)


def update_kernel(target, last, sums_ref, means_ref, price_ref, packed_ref, new_ref, cost_ref):
    width = means_ref.shape[1]
    sums = sums_ref[...].astype(jnp.float32)
    total = jnp.sum(sums, axis=0)
    load = total[:, width : width + 1] + total[:, width + 1 : width + 2] + total[:, width + 2 : width + 3]
    means = (total[:, :width] + prior_mass * means_ref[...]) / (load + prior_mass)
    price = price_ref[...] + price_rate * jnp.log((load + prior_mass) / (target + prior_mass))
    new_ref[...] = means
    cost_ref[...] = price
    if last:
        packed_ref[...] = packed_with(means, price)
    else:
        offset = 0.5 * jnp.sum(means * means, axis=1, keepdims=True) + price
        packed_ref[...] = packed_with(means, offset)


def shards(points, candidates, centroids, prices):
    cells = lax.axis_size("row")
    copies = lax.axis_size("col")
    wanted = candidates[0].T
    tops, count = wanted.shape
    width = points.shape[2]
    centres = centroids.shape[1]
    per_block = points.shape[1] // count
    capacity = max(2, (2 * tops * count + cells - 1) // cells)
    slots = capacity * per_block
    rows = cells * slots
    share = centres // copies
    target = copies * count * per_block / centres
    chunks = 4

    outgoing = pl.pallas_call(
        functools.partial(pack_kernel, cells, capacity, per_block),
        out_shape=jax.ShapeDtypeStruct((rows, width), jnp.bfloat16),
        in_specs=[VMEM, VMEM],
        out_specs=VMEM,
        name="pack",
    )(wanted, points[0])
    incoming = lax.all_to_all(outgoing.reshape(cells, slots, width), "row", 0, 0, tiled=True)
    incoming = incoming.reshape(rows, width)

    price_column = prices[0].reshape(centres, 1)
    packed = pl.pallas_call(
        start_kernel,
        out_shape=jax.ShapeDtypeStruct((centres, width + LANES), jnp.bfloat16),
        in_specs=[VMEM, VMEM],
        out_specs=VMEM,
        name="start",
    )(centroids[0], price_column)
    place = lax.axis_index("col") * share
    means = lax.dynamic_slice_in_dim(centroids[0], place, share, 0)
    price = lax.dynamic_slice_in_dim(price_column, place, share, 0)

    def exchanged(values):
        filled = lax.all_to_all(values.reshape(cells, 1, slots), "row", 0, 0, tiled=True)
        return filled.reshape(cells, slots)

    for sweep_index in range(STEPS):
        last = sweep_index == STEPS - 1
        logs = pl.pallas_call(
            functools.partial(stats_kernel, chunks),
            out_shape=jax.ShapeDtypeStruct((cells, slots), jnp.float32),
            in_specs=[VMEM, VMEM],
            out_specs=VMEM,
            name="stats",
        )(packed, incoming)
        slot_log = pl.pallas_call(
            functools.partial(norm_kernel, per_block, capacity),
            out_shape=jax.ShapeDtypeStruct((cells, slots), jnp.float32),
            in_specs=[VMEM, VMEM],
            out_specs=VMEM,
            name="norm",
        )(wanted, exchanged(logs))
        sums = pl.pallas_call(
            functools.partial(sums_kernel, chunks),
            out_shape=jax.ShapeDtypeStruct((centres, width + LANES), jnp.bfloat16),
            in_specs=[VMEM, VMEM, VMEM],
            out_specs=VMEM,
            name="sums",
        )(packed, incoming, exchanged(slot_log))
        pieces = lax.all_to_all(
            sums.reshape(copies, share, width + LANES), "col", 0, 0, tiled=True
        )
        piece, means, price = pl.pallas_call(
            functools.partial(update_kernel, target, last),
            out_shape=(
                jax.ShapeDtypeStruct((share, width + LANES), jnp.bfloat16),
                jax.ShapeDtypeStruct((share, width), jnp.float32),
                jax.ShapeDtypeStruct((share, 1), jnp.float32),
            ),
            in_specs=[VMEM, VMEM, VMEM],
            out_specs=(VMEM, VMEM, VMEM),
            name="update",
        )(pieces, means, price)
        packed = lax.all_gather(piece, "col", axis=0, tiled=True)

    new_centroids = packed[:, :width].astype(jnp.float32)
    new_prices = jnp.sum(packed[:, width : width + 3].astype(jnp.float32), axis=1)
    return (new_centroids[None], new_prices[None])


def solution(mesh):
    placed = (P("col", "row", None), P("col", "row", None), P("row", None, None), P("row", None))
    return jax.shard_map(
        shards,
        mesh=mesh,
        in_specs=placed,
        out_specs=(P("row", None, None), P("row", None)),
        check_vma=False,
    )
```

time: 430 us -> 309 us (0.72)
  waiting for transfers between devices: 196 us -> 79.1 us
  Pallas kernels: 0 us -> 36.7 us
  other arithmetic: 26.9 us -> 1.61 us
  matrix products: 22.4 us -> 0 us
  starting transfers between devices: 33 us -> 53.1 us
  blocking collectives: 114 us -> 131 us
  local copies, waits for them, and re-layouts: 21.4 us -> 5.38 us
  between operations: 14.3 us -> 0.66 us
    all_gather x2 -> x0, waiting for transfers between devices: 109 us -> none  [over_pieces(): blocks = lax.all_gather(shard, axis)]
    all_to_all x2 -> x5, blocking collectives: 42 us -> 97.8 us  [the longest x4 74.1 us: exchanged(): lax.all_to_all(values.reshape(cells, 1, slots), 'row', 0, 0, tiled=True)]
    all_gather x2, blocking collectives: 72.5 us -> 33.5 us  [shards(): packed = lax.all_gather(piece, 'col', axis=0, tiled=True)]
    pallas_call x0 -> x10, Pallas kernels: none -> 36.7 us  [the longest x2 10.6 us: shards(): pl.pallas_call(functools.partial(sums_kernel, chunks), out_shape=jax.Shap...]
    dot_general x11 -> x0, matrix products: 22.4 us -> none  [the longest x2 8.38 us: shards(): lax.dot_general(weight.astype(jnp.bfloat16), incoming, (((0,), (0,)), (()...]
    all_to_all x3 -> x2, starting transfers between devices: 32.7 us -> 53.1 us  [the longest x1 38.9 us: shards(): lax.all_to_all(sums.reshape(copies, share, width + LANES), 'col', 0, 0, t...]
    reduce_sum x11 -> x1, other arithmetic: 17 us -> 0.68 us  [shards(): new_prices = jnp.sum(packed[:, width:width + 3].astype(jnp.float32), axis=1)]
    another operation x3 -> x1, local copies, waits for them, and re-layouts: 10.3 us -> 0.79 us  [shards(): price_column = prices[0].reshape(centres, 1)]
  transfers between devices with their start and end apart: 5 -> 2, of which waited for: 5 -> 2; matrix products, arithmetic and copies ran while one was open for 2% -> 1% of each run, Pallas kernels for 0% -> 1%
where the time goes in v1:
time: 309 us; the launch traced here: 308 us
  blocking collectives  131 us (42%)
  waiting for transfers between devices  79.1 us (26%)
  starting transfers between devices  53.1 us (17%)
  Pallas kernels  36.7 us (12%)
  local copies, waits for them, and re-layouts  5.38 us (2%)
    all_to_all x4, blocking collectives, exchanged(): lax.all_to_all(values.reshape(cells, 1, slots), 'row', 0, 0, tiled=True)  74.1 us
    all_to_all x1, waiting for transfers between devices, shards(): lax.all_to_all(outgoing.reshape(cells, slots, width), 'row', 0, 0, tiled=...  65.4 us
    all_to_all x1, starting transfers between devices, shards(): lax.all_to_all(sums.reshape(copies, share, width + LANES), 'col', 0, 0, t...  38.9 us
    all_gather x2, blocking collectives, shards(): packed = lax.all_gather(piece, 'col', axis=0, tiled=True)  33.5 us
    all_to_all x1, blocking collectives, shards(): lax.all_to_all(sums.reshape(copies, share, width + LANES), 'col', 0, 0, t...  23.7 us
    all_to_all x1, starting transfers between devices, shards(): lax.all_to_all(outgoing.reshape(cells, slots, width), 'row', 0, 0, tiled=...  14.2 us
    all_to_all x1, waiting for transfers between devices, shards(): lax.all_to_all(sums.reshape(copies, share, width + LANES), 'col', 0, 0, t...  13.7 us
    pallas_call x2, Pallas kernels, shards(): pl.pallas_call(functools.partial(sums_kernel, chunks), out_shape=jax.Shap...  10.6 us
  transfers between devices with their start and end apart: 2, of which 2 were waited for; matrix products, arithmetic and copies ran while one was open for 1% of the time, Pallas kernels for 1%

profile of v1, /device:TPU:1, one launch (start us, length us, event | category | flops | bytes accessed | tf_op | source)
XLA Modules:
  0.0 307.8 jit_solution(14020071347990005081)
XLA Ops:
  0.6 5.1 %pack.1 = bf16[2048,768]{1,0:T(8,128)(2,1)} custom-call(s32[4,32]{1,0:T(4,128)} %bitcast.53, bf16[256,768]{1,0:T(8,128)(2,1)} %bitcast.44), custom_call_target="tpu_custom_call" | custom-call | tf_op jit(solution)/shard_map/pack/pallas_call | solution.py:221
  5.8 14.2 %all-to-all-start = ((bf16[64,32,768]{2,1,0:T(8,128)(2,1)}), bf16[64,32,768]{2,1,0:T(8,128)(2,1)S(1)}, u32[]{:S(2)}, u32[]{:S(2)}) async-start(bf16[64,32,768]{2,1,0:T(8,128)(2,1)} %bitcast.40), calls=%async_computation | async-start | bytes 6291456 | tf_op jit(solution)/shard_map/all_to_all | solution.py:228
  20.8 2.2 start.1.packed_ref
  22.9 65.4 %all-to-all-done = bf16[64,32,768]{2,1,0:T(8,128)(2,1)S(1)} async-done(((bf16[64,32,768]{2,1,0:T(8,128)(2,1)}), bf16[64,32,768]{2,1,0:T(8,128)(2,1)S(1)}, u32[]{:S(2)}, u32[]{:S(2)}) %all-to-all-start) | async-done | bytes 3145760 | tf_op jit(solution)/shard_map/all_to_all | solution.py:228
  88.4 1.6 copy-done
  90.0 5.2 %stats.2 = f32[64,32]{1,0:T(8,128)} custom-call(bf16[256,896]{1,0:T(8,128)(2,1)} %start.1.packed_ref, bf16[2048,768]{1,0:T(8,128)(2,1)} %bitcast.36), custom_call_target="tpu_custom_call" | custom-call | tf_op jit(solution)/shard_map/stats/pallas_call | solution.py:249
  95.3 26.0 %all_to_all.35 = f32[64,1,32]{2,1,0:T(1,128)} all-to-all(f32[64,1,32]{2,1,0:T(1,128)} %bitcast.47), channel_id=1, replica_groups=mesh['row'=64,'col'=16] {'row'}, dimensions={0} | all-to-all | bytes 16384 | tf_op jit(solution)/shard_map/all_to_all | solution.py:244
  121.2 2.2 norm.2
  123.5 16.1 %all_to_all.36 = f32[64,1,32]{2,1,0:T(1,128)} all-to-all(f32[64,1,32]{2,1,0:T(1,128)} %bitcast.50), channel_id=1, replica_groups=mesh['row'=64,'col'=16] {'row'}, dimensions={0} | all-to-all | bytes 16384 | tf_op jit(solution)/shard_map/all_to_all | solution.py:244
  139.6 5.3 %sums.2 = bf16[256,896]{1,0:T(8,128)(2,1)} custom-call(bf16[256,896]{1,0:T(8,128)(2,1)} %start.1.packed_ref, bf16[2048,768]{1,0:T(8,128)(2,1)} %bitcast.37, f32[64,32]{1,0:T(8,128)} %bitcast.46), custom_call_target="tpu_custom_call" | custom-call | tf_op jit(solution)/shard_map/sums/pallas_call | solution.py:263
  144.9 38.9 %all-to-all-start.3 = ((bf16[16,16,896]{2,1,0:T(8,128)(2,1)}), bf16[16,16,896]{2,1,0:T(8,128)(2,1)S(1)}, u32[]{:S(2)}, u32[]{:S(2)}) async-start(bf16[16,16,896]{2,1,0:T(8,128)(2,1)} %bitcast.41), calls=%async_computation.3 | async-start | bytes 917504 | tf_op jit(solution)/shard_map/all_to_all | solution.py:270
  184.6 1.4 dynamic-slice_bitcast_fusion.means_ref
  186.0 13.7 %all-to-all-done.3.sums_ref = bf16[16,16,896]{2,1,0:T(8,128)(2,1)S(1)} async-done(((bf16[16,16,896]{2,1,0:T(8,128)(2,1)}), bf16[16,16,896]{2,1,0:T(8,128)(2,1)S(1)}, u32[]{:S(2)}, u32[]{:S(2)}) %all-to-all-start.3) | async-done | bytes 458784 | tf_op jit(solution)/shard_map/all_to_all | solution.py:270
  200.4 2.0 update.2
  202.4 17.5 %all_gather.6.packed_ref = bf16[256,896]{1,0:T(8,128)(2,1)} all-gather(bf16[16,896]{1,0:T(8,128)(2,1)} %get-tuple-element.6), channel_id=1, replica_groups=mesh['row'=64,'col'=16] {'col'}, dimensions={0}, use_global_device_ids=true | all-gather | bytes 487424 | tf_op jit(solution)/shard_map/all_gather | solution.py:284
  219.9 5.2 %stats.3 = f32[64,32]{1,0:T(8,128)} custom-call(bf16[256,896]{1,0:T(8,128)(2,1)} %all_gather.6.packed_ref, bf16[2048,768]{1,0:T(8,128)(2,1)} %bitcast.38), custom_call_target="tpu_custom_call" | custom-call | tf_op jit(solution)/shard_map/stats/pallas_call | solution.py:249
  225.2 16.0 %all_to_all.37 = f32[64,1,32]{2,1,0:T(1,128)} all-to-all(f32[64,1,32]{2,1,0:T(1,128)} %bitcast.48), channel_id=1, replica_groups=mesh['row'=64,'col'=16] {'row'}, dimensions={0} | all-to-all | bytes 16384 | tf_op jit(solution)/shard_map/all_to_all | solution.py:244
  241.2 2.2 norm.3
  243.4 16.0 %all_to_all.38 = f32[64,1,32]{2,1,0:T(1,128)} all-to-all(f32[64,1,32]{2,1,0:T(1,128)} %bitcast.52), channel_id=1, replica_groups=mesh['row'=64,'col'=16] {'row'}, dimensions={0} | all-to-all | bytes 16384 | tf_op jit(solution)/shard_map/all_to_all | solution.py:244
  259.4 5.3 %sums.3 = bf16[256,896]{1,0:T(8,128)(2,1)} custom-call(bf16[256,896]{1,0:T(8,128)(2,1)} %all_gather.6.packed_ref, bf16[2048,768]{1,0:T(8,128)(2,1)} %bitcast.39, f32[64,32]{1,0:T(8,128)} %bitcast.45), custom_call_target="tpu_custom_call" | custom-call | tf_op jit(solution)/shard_map/sums/pallas_call | solution.py:263
  264.7 23.7 %all_to_all.39.sums_ref = bf16[16,16,896]{2,1,0:T(8,128)(2,1)} all-to-all(bf16[16,16,896]{2,1,0:T(8,128)(2,1)} %bitcast.42), channel_id=1, replica_groups=mesh['row'=64,'col'=16] {'col'}, dimensions={0} | all-to-all | bytes 917504 | tf_op jit(solution)/shard_map/all_to_all | solution.py:270
  288.4 1.9 update.3
  290.2 15.9 %all_gather.7 = bf16[256,896]{1,0:T(8,128)(2,1)S(1)} all-gather(bf16[16,896]{1,0:T(8,128)(2,1)} %get-tuple-element.9), channel_id=1, replica_groups=mesh['row'=64,'col'=16] {'col'}, dimensions={0}, use_global_device_ids=true | all-gather | bytes 487424 | tf_op jit(solution)/shard_map/all_gather | solution.py:284
  306.2 0.9 fusion
  (9 shorter events, 3.0 us)
Async XLA Ops:
  5.8 14.2 %copy-start.2 = (f32[1,256]{1,0:T(1,128)S(1)}, f32[1,256]{1,0:T(1,128)}, u32[]{:S(2)}) copy-start(f32[1,256]{1,0:T(1,128)} %param.7) | copy-start | bytes 3076
  5.8 82.6 %all-to-all-start = ((bf16[64,32,768]{2,1,0:T(8,128)(2,1)}), bf16[64,32,768]{2,1,0:T(8,128)(2,1)S(1)}, u32[]{:S(2)}, u32[]{:S(2)}) async-start(bf16[64,32,768]{2,1,0:T(8,128)(2,1)} %bitcast.40), calls=%async_computation | async-start | bytes 6291456 | tf_op jit(solution)/shard_map/all_to_all | solution.py:228
  88.4 1.7 copy-start
  144.9 54.8 %all-to-all-start.3 = ((bf16[16,16,896]{2,1,0:T(8,128)(2,1)}), bf16[16,16,896]{2,1,0:T(8,128)(2,1)S(1)}, u32[]{:S(2)}, u32[]{:S(2)}) async-start(bf16[16,16,896]{2,1,0:T(8,128)(2,1)} %bitcast.41), calls=%async_computation.3 | async-start | bytes 917504 | tf_op jit(solution)/shard_map/all_to_all | solution.py:270
  199.7 0.8 copy-start.1

commit v2 on v1

--- a/solution.py
+++ b/solution.py
@@ -15,6 +15,25 @@
 empty_log = 1e30
 
 VMEM = pl.BlockSpec(memory_space=pltpu.VMEM)
+
+
+def on_chip(kernel, name, outs, held=None):
+    def run(*args):
+        marks = held or (True,) * len(args)
+        args = [
+            pltpu.with_memory_space_constraint(arg, pltpu.VMEM) if mark else arg
+            for arg, mark in zip(args, marks)
+        ]
+        return pl.pallas_call(
+            kernel,
+            out_shape=outs,
+            in_specs=[VMEM] * len(args),
+            out_specs=(VMEM,) * len(outs) if isinstance(outs, tuple) else VMEM,
+            compiler_params=pltpu.CompilerParams(vmem_limit_bytes=24 << 20),
+            name=name,
+        )(*args)
+
+    return run
 
 
 def iota(shape, dim):
@@ -54,22 +73,20 @@
     wanted = wanted_ref[...]
     count = wanted.shape[1]
     rows = count * per_block
-    total = cells * capacity * per_block
+    chunk = out_ref.shape[0]
     _, named, before = block_names(wanted, cells)
     both = jnp.concatenate([named, before], axis=1)
-    chunk = total // 4
-    for k in range(4):
-        place = iota((chunk, 1), 0) + k * chunk
-        owner = (place // (capacity * per_block) == iota((chunk, cells), 1)).astype(jnp.float32)
-        spread = small_dot(owner, both, ((1,), (0,)))
-        slot = ((place // per_block) % capacity).astype(jnp.float32)
-        chosen = spread[:, :count] * (spread[:, count:] == slot).astype(jnp.float32)
-        block = iota((chunk, count), 1).astype(jnp.float32)
-        source = jnp.sum(chosen * (block + 1.0), axis=1, keepdims=True) - 1.0
-        source = source.astype(jnp.int32) * per_block + place % per_block
-        pick = (iota((chunk, rows), 1) == source).astype(jnp.float32).astype(jnp.bfloat16)
-        moved = jnp.dot(pick, points_ref[...], preferred_element_type=jnp.float32)
-        out_ref[k * chunk : (k + 1) * chunk, :] = moved.astype(jnp.bfloat16)
+    place = iota((chunk, 1), 0) + pl.program_id(0) * chunk
+    owner = (place // (capacity * per_block) == iota((chunk, cells), 1)).astype(jnp.float32)
+    spread = small_dot(owner, both, ((1,), (0,)))
+    slot = ((place // per_block) % capacity).astype(jnp.float32)
+    chosen = spread[:, :count] * (spread[:, count:] == slot).astype(jnp.float32)
+    block = iota((chunk, count), 1).astype(jnp.float32)
+    source = jnp.sum(chosen * (block + 1.0), axis=1, keepdims=True) - 1.0
+    source = source.astype(jnp.int32) * per_block + place % per_block
+    pick = (iota((chunk, rows), 1) == source).astype(jnp.float32).astype(jnp.bfloat16)
+    moved = jnp.dot(pick, points_ref[...], preferred_element_type=jnp.float32)
+    out_ref[...] = moved.astype(jnp.bfloat16)
 
 
 def centre_offset(packed, width):
@@ -181,10 +198,14 @@
     return jnp.concatenate([means.astype(jnp.bfloat16), tail.astype(jnp.bfloat16)], axis=1)
 
 
-def start_kernel(means_ref, price_ref, out_ref):
+def start_kernel(means_ref, price_ref, packed_ref, own_ref, cost_ref):
     means = means_ref[...]
     offset = 0.5 * jnp.sum(means * means, axis=1, keepdims=True) + price_ref[...]
-    out_ref[...] = packed_with(means, offset)
+    packed_ref[...] = packed_with(means, offset)
+    share = own_ref.shape[0]
+    place = pl.multiple_of(lax.axis_index("col") * share, share)
+    own_ref[...] = means_ref[pl.ds(place, share), :]
+    cost_ref[...] = price_ref[pl.ds(place, share), :]
 
 
 def update_kernel(target, last, sums_ref, means_ref, price_ref, packed_ref, new_ref, cost_ref):
@@ -196,11 +217,10 @@
     price = price_ref[...] + price_rate * jnp.log((load + prior_mass) / (target + prior_mass))
     new_ref[...] = means
     cost_ref[...] = price
-    if last:
-        packed_ref[...] = packed_with(means, price)
-    else:
-        offset = 0.5 * jnp.sum(means * means, axis=1, keepdims=True) + price
-        packed_ref[...] = packed_with(means, offset)
+    column = price if last else 0.5 * jnp.sum(means * means, axis=1, keepdims=True) + price
+    packed = packed_with(means, column)
+    for copy in range(packed_ref.shape[0]):
+        packed_ref[copy] = packed
 
 
 def shards(points, candidates, centroids, prices):
@@ -218,27 +238,32 @@
     target = copies * count * per_block / centres
     chunks = 4
 
+    chunk = rows // chunks
     outgoing = pl.pallas_call(
         functools.partial(pack_kernel, cells, capacity, per_block),
         out_shape=jax.ShapeDtypeStruct((rows, width), jnp.bfloat16),
-        in_specs=[VMEM, VMEM],
-        out_specs=VMEM,
+        grid=(chunks,),
+        in_specs=[
+            pl.BlockSpec(wanted.shape, lambda k: (0, 0)),
+            pl.BlockSpec(points.shape[1:], lambda k: (0, 0)),
+        ],
+        out_specs=pl.BlockSpec((chunk, width), lambda k: (k, 0)),
         name="pack",
     )(wanted, points[0])
     incoming = lax.all_to_all(outgoing.reshape(cells, slots, width), "row", 0, 0, tiled=True)
     incoming = incoming.reshape(rows, width)
 
     price_column = prices[0].reshape(centres, 1)
-    packed = pl.pallas_call(
+    packed, means, price = on_chip(
         start_kernel,
-        out_shape=jax.ShapeDtypeStruct((centres, width + LANES), jnp.bfloat16),
-        in_specs=[VMEM, VMEM],
-        out_specs=VMEM,
-        name="start",
+        "start",
+        (
+            jax.ShapeDtypeStruct((centres, width + LANES), jnp.bfloat16),
+            jax.ShapeDtypeStruct((share, width), jnp.float32),
+            jax.ShapeDtypeStruct((share, 1), jnp.float32),
+        ),
+        (False, False),
     )(centroids[0], price_column)
-    place = lax.axis_index("col") * share
-    means = lax.dynamic_slice_in_dim(centroids[0], place, share, 0)
-    price = lax.dynamic_slice_in_dim(price_column, place, share, 0)
 
     def exchanged(values):
         filled = lax.all_to_all(values.reshape(cells, 1, slots), "row", 0, 0, tiled=True)
@@ -246,42 +271,37 @@
 
     for sweep_index in range(STEPS):
         last = sweep_index == STEPS - 1
-        logs = pl.pallas_call(
+        logs = on_chip(
             functools.partial(stats_kernel, chunks),
-            out_shape=jax.ShapeDtypeStruct((cells, slots), jnp.float32),
-            in_specs=[VMEM, VMEM],
-            out_specs=VMEM,
-            name="stats",
+            "stats",
+            jax.ShapeDtypeStruct((cells, slots), jnp.float32),
+            (sweep_index > 0, True),
         )(packed, incoming)
-        slot_log = pl.pallas_call(
+        slot_log = on_chip(
             functools.partial(norm_kernel, per_block, capacity),
-            out_shape=jax.ShapeDtypeStruct((cells, slots), jnp.float32),
-            in_specs=[VMEM, VMEM],
-            out_specs=VMEM,
-            name="norm",
+            "norm",
+            jax.ShapeDtypeStruct((cells, slots), jnp.float32),
         )(wanted, exchanged(logs))
-        sums = pl.pallas_call(
+        sums = on_chip(
             functools.partial(sums_kernel, chunks),
-            out_shape=jax.ShapeDtypeStruct((centres, width + LANES), jnp.bfloat16),
-            in_specs=[VMEM, VMEM, VMEM],
-            out_specs=VMEM,
-            name="sums",
+            "sums",
+            jax.ShapeDtypeStruct((centres, width + LANES), jnp.bfloat16),
+            (sweep_index > 0, True, True),
         )(packed, incoming, exchanged(slot_log))
         pieces = lax.all_to_all(
             sums.reshape(copies, share, width + LANES), "col", 0, 0, tiled=True
         )
-        piece, means, price = pl.pallas_call(
+        piece, means, price = on_chip(
             functools.partial(update_kernel, target, last),
-            out_shape=(
-                jax.ShapeDtypeStruct((share, width + LANES), jnp.bfloat16),
+            "update",
+            (
+                jax.ShapeDtypeStruct((copies, share, width + LANES), jnp.bfloat16),
                 jax.ShapeDtypeStruct((share, width), jnp.float32),
                 jax.ShapeDtypeStruct((share, 1), jnp.float32),
             ),
-            in_specs=[VMEM, VMEM, VMEM],
-            out_specs=(VMEM, VMEM, VMEM),
-            name="update",
+            (True, False, False),
         )(pieces, means, price)
-        packed = lax.all_gather(piece, "col", axis=0, tiled=True)
+        packed = lax.all_to_all(piece, "col", 0, 0, tiled=True).reshape(centres, width + LANES)
 
     new_centroids = packed[:, :width].astype(jnp.float32)
     new_prices = jnp.sum(packed[:, width : width + 3].astype(jnp.float32), axis=1)

time: 309 us -> 288 us (0.932)
  blocking collectives: 131 us -> 182 us
  starting transfers between devices: 53.1 us -> 14.2 us
  Pallas kernels: 36.7 us -> 19.4 us
  waiting for transfers between devices: 79.1 us -> 66.1 us
    all_to_all x1 -> x2, blocking collectives: 23.7 us -> 75.7 us  [shards(): lax.all_to_all(sums.reshape(copies, share, width + LANES), 'col', 0, 0, t...]
    all_to_all x1 -> x0, starting transfers between devices: 38.9 us -> none  [shards(): lax.all_to_all(sums.reshape(copies, share, width + LANES), 'col', 0, 0, t...]
    all_to_all x0 -> x2, blocking collectives: none -> 37.1 us  [shards(): lax.all_to_all(piece, 'col', 0, 0, tiled=True)]
    all_gather x2 -> x0, blocking collectives: 33.5 us -> none  [shards(): packed = lax.all_gather(piece, 'col', axis=0, tiled=True)]
    pallas_call x9, Pallas kernels: 31.5 us -> 13.3 us  [run(): pl.pallas_call(kernel, out_shape=outs, in_specs=[VMEM] * len(args), out_s...]
    all_to_all x1 -> x0, waiting for transfers between devices: 13.7 us -> none  [shards(): lax.all_to_all(sums.reshape(copies, share, width + LANES), 'col', 0, 0, t...]
    all_to_all x4, blocking collectives: 74.1 us -> 69.6 us  [exchanged(): lax.all_to_all(values.reshape(cells, 1, slots), 'row', 0, 0, tiled=True)]
  transfers between devices with their start and end apart: 2 -> 1, of which waited for: 2 -> 1; matrix products, arithmetic and copies ran while one was open for 1% -> 0% of each run, Pallas kernels for 1% -> 0%
where the time goes in v2:
time: 288 us
  blocking collectives  182 us (63%)
  waiting for transfers between devices  66.1 us (23%)
  Pallas kernels  19.4 us (7%)
  starting transfers between devices  14.2 us (5%)
  local copies, waits for them, and re-layouts  3.06 us (1%)
    all_to_all x2, blocking collectives, shards(): lax.all_to_all(sums.reshape(copies, share, width + LANES), 'col', 0, 0, t...  75.7 us
    all_to_all x4, blocking collectives, exchanged(): lax.all_to_all(values.reshape(cells, 1, slots), 'row', 0, 0, tiled=True)  69.6 us
    all_to_all x1, waiting for transfers between devices, shards(): lax.all_to_all(outgoing.reshape(cells, slots, width), 'row', 0, 0, tiled=...  66.1 us
    all_to_all x2, blocking collectives, shards(): lax.all_to_all(piece, 'col', 0, 0, tiled=True)  37.1 us
    all_to_all x1, starting transfers between devices, shards(): lax.all_to_all(outgoing.reshape(cells, slots, width), 'row', 0, 0, tiled=...  14.2 us
    pallas_call x9, Pallas kernels, run(): pl.pallas_call(kernel, out_shape=outs, in_specs=[VMEM] * len(args), out_s...  13.3 us
    pallas_call x1, Pallas kernels, shards(): pl.pallas_call(functools.partial(pack_kernel, cells, capacity, per_block)...  6.16 us
  transfers between devices with their start and end apart: 1, of which 1 were waited for; matrix products, arithmetic and copies ran while one was open for 0% of the time, Pallas kernels for 0%

profile of v2, /device:TPU:1, one launch (start us, length us, event | category | flops | bytes accessed | tf_op | source)
XLA Modules:
  0.0 287.5 jit_solution(2262168839119062356)
XLA Ops:
  0.6 6.2 %pack.1 = bf16[2048,768]{1,0:T(8,128)(2,1)} custom-call(s32[4,32]{1,0:T(4,128)} %bitcast.51, bf16[256,768]{1,0:T(8,128)(2,1)} %bitcast.57), custom_call_target="tpu_custom_call" | custom-call | tf_op jit(solution)/shard_map/pack/pallas_call | solution.py:242
  6.8 14.2 %all-to-all-start = ((bf16[64,32,768]{2,1,0:T(8,128)(2,1)}), bf16[64,32,768]{2,1,0:T(8,128)(2,1)S(1)}, u32[]{:S(2)}, u32[]{:S(2)}) async-start(bf16[64,32,768]{2,1,0:T(8,128)(2,1)} %bitcast.54), calls=%async_computation | async-start | bytes 6291456 | tf_op jit(solution)/shard_map/all_to_all | solution.py:253
  21.1 1.1 copy-done.3
  22.5 0.8 copy-done
  23.3 66.1 %all-to-all-done = bf16[64,32,768]{2,1,0:T(8,128)(2,1)S(1)} async-done(((bf16[64,32,768]{2,1,0:T(8,128)(2,1)}), bf16[64,32,768]{2,1,0:T(8,128)(2,1)S(1)}, u32[]{:S(2)}, u32[]{:S(2)}) %all-to-all-start) | async-done | bytes 3145760 | tf_op jit(solution)/shard_map/all_to_all | solution.py:253
  89.4 1.0 copy-done.1
  90.4 2.6 stats.2
  93.0 25.6 %all_to_all.45 = f32[64,1,32]{2,1,0:T(1,128)S(1)} all-to-all(f32[64,1,32]{2,1,0:T(1,128)S(1)} %bitcast.45), channel_id=1, replica_groups=mesh['row'=64,'col'=16] {'row'}, dimensions={0} | all-to-all | bytes 16384 | tf_op jit(solution)/shard_map/all_to_all | solution.py:269
  118.6 0.8 norm.2
  119.4 14.7 %all_to_all.46 = f32[64,1,32]{2,1,0:T(1,128)S(1)} all-to-all(f32[64,1,32]{2,1,0:T(1,128)S(1)} %bitcast.48), channel_id=1, replica_groups=mesh['row'=64,'col'=16] {'row'}, dimensions={0} | all-to-all | bytes 16384 | tf_op jit(solution)/shard_map/all_to_all | solution.py:269
  134.1 2.5 sums.2
  136.6 54.8 %all_to_all.47.sums_ref = bf16[16,16,896]{2,1,0:T(8,128)(2,1)S(1)} all-to-all(bf16[16,16,896]{2,1,0:T(8,128)(2,1)S(1)} %bitcast.41), channel_id=1, replica_groups=mesh['row'=64,'col'=16] {'col'}, dimensions={0} | all-to-all | bytes 917504 | tf_op jit(solution)/shard_map/all_to_all | solution.py:291
  191.4 0.3 update.2
  191.8 18.6 %all_to_all.48 = bf16[16,16,896]{2,1,0:T(8,128)(2,1)S(1)} all-to-all(bf16[16,16,896]{2,1,0:T(8,128)(2,1)S(1)} %get-tuple-element.12), channel_id=1, replica_groups=mesh['row'=64,'col'=16] {'col'}, dimensions={0} | all-to-all | bytes 917504 | tf_op jit(solution)/shard_map/all_to_all | solution.py:304
  210.3 2.6 stats.3
  212.9 14.7 %all_to_all.49 = f32[64,1,32]{2,1,0:T(1,128)S(1)} all-to-all(f32[64,1,32]{2,1,0:T(1,128)S(1)} %bitcast.46), channel_id=1, replica_groups=mesh['row'=64,'col'=16] {'row'}, dimensions={0} | all-to-all | bytes 16384 | tf_op jit(solution)/shard_map/all_to_all | solution.py:269
  227.6 0.8 norm.3
  228.4 14.7 %all_to_all.50 = f32[64,1,32]{2,1,0:T(1,128)S(1)} all-to-all(f32[64,1,32]{2,1,0:T(1,128)S(1)} %bitcast.50), channel_id=1, replica_groups=mesh['row'=64,'col'=16] {'row'}, dimensions={0} | all-to-all | bytes 16384 | tf_op jit(solution)/shard_map/all_to_all | solution.py:269
  243.1 2.5 sums.3
  245.7 20.9 %all_to_all.51.sums_ref = bf16[16,16,896]{2,1,0:T(8,128)(2,1)S(1)} all-to-all(bf16[16,16,896]{2,1,0:T(8,128)(2,1)S(1)} %bitcast.40), channel_id=1, replica_groups=mesh['row'=64,'col'=16] {'col'}, dimensions={0} | all-to-all | bytes 917504 | tf_op jit(solution)/shard_map/all_to_all | solution.py:291
  266.5 0.8 update.3
  267.3 18.6 %all_to_all.52 = bf16[16,16,896]{2,1,0:T(8,128)(2,1)S(1)} all-to-all(bf16[16,16,896]{2,1,0:T(8,128)(2,1)S(1)} %get-tuple-element.15), channel_id=1, replica_groups=mesh['row'=64,'col'=16] {'col'}, dimensions={0} | all-to-all | bytes 917504 | tf_op jit(solution)/shard_map/all_to_all | solution.py:304
  285.9 0.9 fusion
  286.8 0.7 convert_reduce_fusion
  (11 shorter events, 0.4 us)
Async XLA Ops:
  6.8 14.2 %copy-start.5 = (f32[1,256]{1,0:T(1,128)S(1)}, f32[1,256]{1,0:T(1,128)}, u32[]{:S(2)}) copy-start(f32[1,256]{1,0:T(1,128)} %param.7) | copy-start | bytes 3076
  6.8 82.6 %all-to-all-start = ((bf16[64,32,768]{2,1,0:T(8,128)(2,1)}), bf16[64,32,768]{2,1,0:T(8,128)(2,1)S(1)}, u32[]{:S(2)}, u32[]{:S(2)}) async-start(bf16[64,32,768]{2,1,0:T(8,128)(2,1)} %bitcast.54), calls=%async_computation | async-start | bytes 6291456 | tf_op jit(solution)/shard_map/all_to_all | solution.py:253
  20.9 97.6 %copy-start.4 = (s32[1,32,4]{1,2,0:T(4,128)S(1)}, s32[1,32,4]{1,2,0:T(4,128)}, u32[]{:S(2)}) copy-start(s32[1,32,4]{1,2,0:T(4,128)} %param.5) | copy-start | bytes 1540
  21.1 1.1 copy-start.3
  22.5 0.8 copy-start
  89.4 1.0 copy-start.1
  90.4 43.7 %copy-start.2 = (bf16[256,896]{1,0:T(8,128)(2,1)S(1)}, bf16[256,896]{1,0:T(8,128)(2,1)}, u32[]{:S(2)}) copy-start(bf16[256,896]{1,0:T(8,128)(2,1)} %copy-done) | copy-start | bytes 1376260

commit v3 on v2

--- a/solution.py
+++ b/solution.py
@@ -9,6 +9,7 @@
 
 STEPS = 2
 LANES = 128
+PARTS = 4
 
 prior_mass = 1.0
 price_rate = 0.5
@@ -69,24 +70,86 @@
     return hot, named, before
 
 
-def pack_kernel(cells, capacity, per_block, wanted_ref, points_ref, out_ref):
+def pack_kernel(cells, capacity, per_block, wanted_ref, points_ref, out_ref, held_ref, sems):
     wanted = wanted_ref[...]
     count = wanted.shape[1]
     rows = count * per_block
-    chunk = out_ref.shape[0]
+    chunks, chunk = held_ref.shape[:2]
     _, named, before = block_names(wanted, cells)
     both = jnp.concatenate([named, before], axis=1)
-    place = iota((chunk, 1), 0) + pl.program_id(0) * chunk
-    owner = (place // (capacity * per_block) == iota((chunk, cells), 1)).astype(jnp.float32)
-    spread = small_dot(owner, both, ((1,), (0,)))
-    slot = ((place // per_block) % capacity).astype(jnp.float32)
-    chosen = spread[:, :count] * (spread[:, count:] == slot).astype(jnp.float32)
-    block = iota((chunk, count), 1).astype(jnp.float32)
-    source = jnp.sum(chosen * (block + 1.0), axis=1, keepdims=True) - 1.0
-    source = source.astype(jnp.int32) * per_block + place % per_block
-    pick = (iota((chunk, rows), 1) == source).astype(jnp.float32).astype(jnp.bfloat16)
-    moved = jnp.dot(pick, points_ref[...], preferred_element_type=jnp.float32)
-    out_ref[...] = moved.astype(jnp.bfloat16)
+    copies = []
+    for k in range(chunks):
+        place = iota((chunk, 1), 0) + k * chunk
+        owner = (place // (capacity * per_block) == iota((chunk, cells), 1)).astype(jnp.float32)
+        spread = small_dot(owner, both, ((1,), (0,)))
+        slot = ((place // per_block) % capacity).astype(jnp.float32)
+        chosen = spread[:, :count] * (spread[:, count:] == slot).astype(jnp.float32)
+        block = iota((chunk, count), 1).astype(jnp.float32)
+        source = jnp.sum(chosen * (block + 1.0), axis=1, keepdims=True) - 1.0
+        source = source.astype(jnp.int32) * per_block + place % per_block
+        pick = (iota((chunk, rows), 1) == source).astype(jnp.float32).astype(jnp.bfloat16)
+        moved = jnp.dot(pick, points_ref[...], preferred_element_type=jnp.float32)
+        held_ref[k] = moved.astype(jnp.bfloat16)
+        copies.append(
+            pltpu.make_async_copy(
+                held_ref.at[k], out_ref.at[pl.ds(k * chunk, chunk)], sems.at[k]
+            )
+        )
+        copies[-1].start()
+    for copy in copies:
+        copy.wait()
+
+
+def index_kernel(capacity, per_block, tops, names_ref, hot_ref, mask_ref, empty_ref):
+    total, lanes = names_ref.shape
+    devices = total // PARTS
+    count = lanes // tops
+    cells = names_ref[pl.ds(1, devices, stride=PARTS), :]
+    slots = names_ref[pl.ds(2, devices, stride=PARTS), :]
+    mine = cells == lax.axis_index("row").astype(jnp.float32)
+    to_block = (iota((lanes, count), 0) % count == iota((lanes, count), 1)).astype(jnp.float32)
+    to_top = (iota((lanes, tops), 0) // count == iota((lanes, tops), 1)).astype(jnp.float32)
+    found_cells, found_slots, found = [], [], []
+    for s in range(capacity):
+        at = jnp.where(mine, jnp.where(slots == s, 1.0, 0.0), 0.0)
+        block = small_dot(at, to_block, ((1,), (0,)))
+        block = jnp.concatenate([block] * tops, axis=1)
+        found_cells.append(small_dot(block * cells, to_top, ((1,), (0,))))
+        found_slots.append(small_dot(block * slots, to_top, ((1,), (0,))))
+        found.append(small_dot(at, jnp.ones((lanes, tops), jnp.float32), ((1,), (0,))))
+    table = jnp.concatenate(found_cells + found_slots + found, axis=1)
+    span = capacity * tops
+    together = LANES // (capacity * per_block)
+    size = hot_ref.shape[0]
+    step = together * capacity
+    row = iota((size, 1), 0)
+    inside = (row % step) // capacity
+    device = row // (step * tops) * together + inside
+    pick = (device == iota((size, devices), 1)).astype(jnp.float32)
+    entry = small_dot(pick, table, ((1,), (0,)))
+    lane = iota(entry.shape, 1)
+    column = (row % capacity) * tops + (row // step) % tops
+
+    def entry_at(start):
+        return jnp.sum(jnp.where(lane == start + column, entry, 0.0), axis=1, keepdims=True)
+
+    cell, slot, there = entry_at(0), entry_at(span), entry_at(2 * span) > 0
+    spot = iota((size, LANES), 1)
+    hot = jnp.where(there, jnp.where(spot.astype(jnp.float32) == cell, 1.0, 0.0), 0.0)
+    hot_ref[...] = hot.astype(jnp.bfloat16)
+    place = inside * capacity + slot.astype(jnp.int32)
+    mask = jnp.where(there, jnp.where(spot // per_block == place, 1.0, 0.0), 0.0)
+    mask_ref[...] = mask.astype(jnp.bfloat16)
+    full = jnp.where(there, 1.0, 0.0)
+    for g in range(size // (step * tops)):
+        head = full[g * step * tops : g * step * tops + step]
+        empty_ref[g * step : (g + 1) * step, :] = jnp.broadcast_to(1.0 - head, (step, LANES))
+
+
+def pair_place(at, copies):
+    core = lax.axis_index("col") % 2
+    half = copies // 2
+    return 2 * at + core if at < half else 2 * (at - half) + 1 - core
 
 
 def centre_offset(packed, width):
@@ -104,30 +167,31 @@
     )
 
 
-def stats_kernel(chunks, packed_ref, incoming_ref, out_ref):
+def row_logs(half, offset, rows):
+    scores = score_chunk(half, offset, rows)
+    highest = jnp.max(scores, axis=0, keepdims=True)
+    return highest + jnp.log(jnp.sum(jnp.exp(scores - highest), axis=0, keepdims=True))
+
+
+def slot_stats_kernel(chunks, packed_ref, incoming_ref, out_ref):
     width = incoming_ref.shape[1]
     packed = packed_ref[...]
     half = packed[:, :width]
     offset = centre_offset(packed, width)
     size = incoming_ref.shape[0] // chunks
-    per_owner = out_ref.shape[1]
-    part = size // per_owner
-    own = iota((part, size), 1) // per_owner == iota((part, size), 0)
-    fold = (iota((size, per_owner), 0) % per_owner == iota((size, per_owner), 1)).astype(
-        jnp.float32
-    )
+    slots = out_ref.shape[1]
+    part = size // slots
     for k in range(chunks):
-        scores = score_chunk(half, offset, incoming_ref[k * size : (k + 1) * size, :])
-        highest = jnp.max(scores, axis=0, keepdims=True)
-        mass = jnp.sum(jnp.exp(scores - highest), axis=0, keepdims=True)
-        logs = jnp.where(own, highest + jnp.log(mass), 0.0)
-        out_ref[k * part : (k + 1) * part, :] = exact_dot(logs, fold, ((1,), (0,)))
+        logs = row_logs(half, offset, incoming_ref[k * size : (k + 1) * size, :])
+        for o in range(part):
+            out_ref[k * part + o : k * part + o + 1, :] = logs[:, o * slots : (o + 1) * slots]
 
 
 def norm_kernel(per_block, capacity, wanted_ref, back_ref, out_ref):
     back = back_ref[...]
     cells = back.shape[0]
-    hots, _, before = block_names(wanted_ref[...], cells)
+    wanted = wanted_ref[...]
+    hots, _, before = block_names(wanted, cells)
     tops = len(hots)
     count = hots[0].shape[1]
     hot = jnp.concatenate(hots, axis=1)
@@ -149,34 +213,118 @@
     norm = jnp.where(in_slot, jnp.concatenate([norm] * tops, axis=0), 0.0)
     value = exact_dot(hot, norm, ((1,), (0,)))
     filled = small_dot(hot, in_slot.astype(jnp.float32), ((1,), (0,)))
-    out_ref[...] = jnp.where(filled > 0, value, empty_log)
-
-
-def sums_kernel(chunks, packed_ref, incoming_ref, log_ref, out_ref):
+    value = jnp.where(filled > 0, value, empty_log)
+    value = jnp.concatenate([value] * (out_ref.shape[2] // value.shape[1]), axis=1)
+    out_ref[:, 0, :] = value
+    names = [wanted[t : t + 1, :].astype(jnp.float32) for t in range(tops)]
+    places = [jnp.sum(one * before, axis=0, keepdims=True) for one in hots]
+    out_ref[:, 1, :] = jnp.broadcast_to(jnp.concatenate(names, axis=1), value.shape)
+    out_ref[:, 2, :] = jnp.broadcast_to(jnp.concatenate(places, axis=1), value.shape)
+    out_ref[:, 3, :] = jnp.zeros(value.shape, jnp.float32)
+
+
+def stats_kernel(chunks, mine_ref, other_ref, incoming_ref, out_ref):
+    width = incoming_ref.shape[1]
+    packed = jnp.concatenate([mine_ref[...], other_ref[...]], axis=0)
+    half = packed[:, :width]
+    offset = centre_offset(packed, width)
+    size = incoming_ref.shape[0] // chunks
+    part = size // LANES
+    for k in range(chunks):
+        logs = row_logs(half, offset, incoming_ref[k * size : (k + 1) * size, :])
+        logs = jnp.concatenate(
+            [logs[:, i * LANES : (i + 1) * LANES] for i in range(part)], axis=0
+        )
+        for o in range(out_ref.shape[0]):
+            out_ref[o, k * part : (k + 1) * part, :] = logs
+
+
+def slot_sums_kernel(chunks, per_owner, packed_ref, incoming_ref, log_ref, out_ref):
     width = incoming_ref.shape[1]
     packed = packed_ref[...]
     half = packed[:, :width]
     offset = centre_offset(packed, width)
     centres = packed.shape[0]
     size = incoming_ref.shape[0] // chunks
-    per_owner = log_ref.shape[1]
     part = size // per_owner
-    own = iota((part, size), 1) // per_owner == iota((part, size), 0)
-    fold = (iota((per_owner, size), 1) % per_owner == iota((per_owner, size), 0)).astype(
-        jnp.float32
-    )
     total = jnp.zeros((centres, width), jnp.float32)
     load = jnp.zeros((centres, 1), jnp.float32)
     for k in range(chunks):
         rows = incoming_ref[k * size : (k + 1) * size, :]
-        logs = exact_dot(log_ref[k * part : (k + 1) * part, :], fold, ((1,), (0,)))
-        logs = jnp.sum(jnp.where(own, logs, 0.0), axis=0, keepdims=True)
+        places = [(k * part + o) * PARTS for o in range(part)]
+        logs = jnp.concatenate([log_ref[p : p + 1, :per_owner] for p in places], axis=1)
         weight = jnp.exp(score_chunk(half, offset, rows) - logs)
         load = load + jnp.sum(weight, axis=1, keepdims=True)
         total = total + jnp.dot(
             weight.astype(jnp.bfloat16), rows, preferred_element_type=jnp.float32
         )
     out_ref[...] = packed_with(total, load)
+
+
+def sums_kernel(
+    chunks,
+    tops,
+    per_block,
+    mine_ref,
+    other_ref,
+    incoming_ref,
+    logs_ref,
+    hot_ref,
+    mask_ref,
+    empty_ref,
+    out_ref,
+):
+    width = incoming_ref.shape[1]
+    packed = jnp.concatenate([mine_ref[...], other_ref[...]], axis=0)
+    half = packed[:, :width]
+    offset = centre_offset(packed, width)
+    centres = packed.shape[0]
+    size = incoming_ref.shape[0] // chunks
+    part = size // LANES
+    groups = incoming_ref.shape[0] // LANES
+    cells = logs_ref.shape[0] // groups
+    step = empty_ref.shape[0] // groups
+
+    def group_logs(g):
+        logs = logs_ref[pl.ds(g, cells, stride=groups), :]
+        high = logs.astype(jnp.bfloat16)
+        rest = logs - high.astype(jnp.float32)
+        middle = rest.astype(jnp.bfloat16)
+        low = (rest - middle.astype(jnp.float32)).astype(jnp.bfloat16)
+        here = pl.ds(g * step * tops, step * tops)
+        found = jnp.dot(
+            hot_ref[here, :cells],
+            jnp.concatenate([high, middle, low], axis=1),
+            preferred_element_type=jnp.float32,
+        )
+        found = found[:, :LANES] + found[:, LANES : 2 * LANES] + found[:, 2 * LANES :]
+        found = jnp.where(mask_ref[here, :].astype(jnp.float32) > 0, found, 0.0)
+        shift = per_block
+        while shift < LANES:
+            found = found + pltpu.roll(found, shift, 1)
+            shift *= 2
+        parts = [found[t * step : (t + 1) * step] for t in range(tops)]
+        largest = functools.reduce(jnp.maximum, parts)
+        mass = functools.reduce(jnp.add, [jnp.exp(one - largest) for one in parts])
+        norm = largest + jnp.log(mass)
+        norm = jnp.where(empty_ref[pl.ds(g * step, step), :] > 0, empty_log, norm)
+        own = iota((step, LANES), 0) == iota((step, LANES), 1) // per_block
+        return jnp.sum(jnp.where(own, norm, 0.0), axis=0, keepdims=True)
+
+    total = jnp.zeros((centres, width), jnp.float32)
+    load = jnp.zeros((centres, 1), jnp.float32)
+    for k in range(chunks):
+        rows = incoming_ref[k * size : (k + 1) * size, :]
+        logs = jnp.concatenate([group_logs(k * part + i) for i in range(part)], axis=1)
+        weight = jnp.exp(score_chunk(half, offset, rows) - logs)
+        load = load + jnp.sum(weight, axis=1, keepdims=True)
+        total = total + jnp.dot(
+            weight.astype(jnp.bfloat16), rows, preferred_element_type=jnp.float32
+        )
+    full = packed_with(total, load)
+    share = out_ref.shape[1]
+    for at in range(out_ref.shape[0]):
+        out_ref[pair_place(at, out_ref.shape[0])] = full[at * share : (at + 1) * share]
 
 
 def packed_with(means, column):
@@ -223,6 +371,24 @@
         packed_ref[copy] = packed
 
 
+def finish_kernel(mine_ref, other_ref, means_ref, price_ref):
+    width = means_ref.shape[1]
+    half, share = mine_ref.shape[:2]
+    swapped = lax.axis_index("col") % 2 > 0
+    for z in range(half):
+        mine, other = mine_ref[z].astype(jnp.float32), other_ref[z].astype(jnp.float32)
+        for at, part in enumerate(
+            (jnp.where(swapped, other, mine), jnp.where(swapped, mine, other))
+        ):
+            first = (2 * z + at) * share
+            means_ref[first : first + share, :] = part[:, :width]
+            price = part[:, width : width + 1] + part[:, width + 1 : width + 2]
+            price = price + part[:, width + 2 : width + 3]
+            here = iota((share, share), 0) == iota((share, share), 1)
+            price = jnp.sum(jnp.where(here, price, 0.0), axis=0, keepdims=True)
+            price_ref[:, first : first + share] = price
+
+
 def shards(points, candidates, centroids, prices):
     cells = lax.axis_size("row")
     copies = lax.axis_size("col")
@@ -242,12 +408,12 @@
     outgoing = pl.pallas_call(
         functools.partial(pack_kernel, cells, capacity, per_block),
         out_shape=jax.ShapeDtypeStruct((rows, width), jnp.bfloat16),
-        grid=(chunks,),
-        in_specs=[
-            pl.BlockSpec(wanted.shape, lambda k: (0, 0)),
-            pl.BlockSpec(points.shape[1:], lambda k: (0, 0)),
+        in_specs=[VMEM, VMEM],
+        out_specs=pl.BlockSpec(memory_space=pl.ANY),
+        scratch_shapes=[
+            pltpu.VMEM((chunks, chunk, width), jnp.bfloat16),
+            pltpu.SemaphoreType.DMA((chunks,)),
         ],
-        out_specs=pl.BlockSpec((chunk, width), lambda k: (k, 0)),
         name="pack",
     )(wanted, points[0])
     incoming = lax.all_to_all(outgoing.reshape(cells, slots, width), "row", 0, 0, tiled=True)
@@ -265,47 +431,80 @@
         (False, False),
     )(centroids[0], price_column)
 
-    def exchanged(values):
-        filled = lax.all_to_all(values.reshape(cells, 1, slots), "row", 0, 0, tiled=True)
-        return filled.reshape(cells, slots)
-
+    sums_shape = jax.ShapeDtypeStruct((centres, width + LANES), jnp.bfloat16)
     for sweep_index in range(STEPS):
         last = sweep_index == STEPS - 1
-        logs = on_chip(
-            functools.partial(stats_kernel, chunks),
-            "stats",
-            jax.ShapeDtypeStruct((cells, slots), jnp.float32),
-            (sweep_index > 0, True),
-        )(packed, incoming)
-        slot_log = on_chip(
-            functools.partial(norm_kernel, per_block, capacity),
-            "norm",
-            jax.ShapeDtypeStruct((cells, slots), jnp.float32),
-        )(wanted, exchanged(logs))
-        sums = on_chip(
-            functools.partial(sums_kernel, chunks),
-            "sums",
-            jax.ShapeDtypeStruct((centres, width + LANES), jnp.bfloat16),
-            (sweep_index > 0, True, True),
-        )(packed, incoming, exchanged(slot_log))
+        if sweep_index == 0:
+            logs = on_chip(
+                functools.partial(slot_stats_kernel, chunks),
+                "stats",
+                jax.ShapeDtypeStruct((cells, slots), jnp.float32),
+                (False, True),
+            )(packed, incoming)
+            logs = lax.all_to_all(logs.reshape(cells, 1, slots), "row", 0, 0, tiled=True)
+            norms = on_chip(
+                functools.partial(norm_kernel, per_block, capacity),
+                "norm",
+                jax.ShapeDtypeStruct((cells, PARTS, tops * count), jnp.float32),
+            )(wanted, logs.reshape(cells, slots))
+            norms = lax.all_to_all(norms, "row", 0, 0, tiled=True).reshape(-1, tops * count)
+            sums = on_chip(
+                functools.partial(slot_sums_kernel, chunks, slots), "sums", sums_shape, (False, True, True)
+            )(packed, incoming, norms)
+            hot, mask, empty = on_chip(
+                functools.partial(index_kernel, capacity, per_block, tops),
+                "index",
+                (
+                    jax.ShapeDtypeStruct((rows // per_block * tops, LANES), jnp.bfloat16),
+                    jax.ShapeDtypeStruct((rows // per_block * tops, LANES), jnp.bfloat16),
+                    jax.ShapeDtypeStruct((rows // per_block, LANES), jnp.float32),
+                ),
+            )(norms)
+            sums, hot, mask, empty = lax.optimization_barrier((sums, hot, mask, empty))
+        else:
+            logs = on_chip(
+                functools.partial(stats_kernel, chunks),
+                "stats_all",
+                jax.ShapeDtypeStruct((cells, rows // LANES, LANES), jnp.float32),
+            )(mine, other, incoming)
+            logs = lax.all_to_all(logs, "row", 0, 0, tiled=True).reshape(-1, LANES)
+            sums = on_chip(
+                functools.partial(sums_kernel, chunks, tops, per_block),
+                "sums_all",
+                jax.ShapeDtypeStruct((copies, share, width + LANES), jnp.bfloat16),
+            )(mine, other, incoming, logs, hot, mask, empty)
         pieces = lax.all_to_all(
             sums.reshape(copies, share, width + LANES), "col", 0, 0, tiled=True
         )
+        half = copies // 2
+        piece_shape = (half if last else 1, share, width + LANES)
         piece, means, price = on_chip(
             functools.partial(update_kernel, target, last),
             "update",
             (
-                jax.ShapeDtypeStruct((copies, share, width + LANES), jnp.bfloat16),
+                jax.ShapeDtypeStruct(piece_shape, jnp.bfloat16),
                 jax.ShapeDtypeStruct((share, width), jnp.float32),
                 jax.ShapeDtypeStruct((share, 1), jnp.float32),
             ),
             (True, False, False),
         )(pieces, means, price)
-        packed = lax.all_to_all(piece, "col", 0, 0, tiled=True).reshape(centres, width + LANES)
-
-    new_centroids = packed[:, :width].astype(jnp.float32)
-    new_prices = jnp.sum(packed[:, width : width + 3].astype(jnp.float32), axis=1)
-    return (new_centroids[None], new_prices[None])
+        groups = [list(range(0, copies, 2)), list(range(1, copies, 2))]
+        pairs = [(i, i ^ 1) for i in range(copies)]
+        if last:
+            mine = lax.all_to_all(piece, "col", 0, 0, axis_index_groups=groups, tiled=True)
+        else:
+            mine = lax.all_gather(piece[0], "col", axis=0, axis_index_groups=groups, tiled=True)
+        other = lax.ppermute(mine, "col", pairs)
+
+    new_centroids, new_prices = on_chip(
+        finish_kernel,
+        "finish",
+        (
+            jax.ShapeDtypeStruct((centres, width), jnp.float32),
+            jax.ShapeDtypeStruct((1, centres), jnp.float32),
+        ),
+    )(mine, other)
+    return (new_centroids[None], new_prices)
 
 
 def solution(mesh):

time: 288 us -> 286 us (level)
  blocking collectives: 182 us -> 172 us
  starting transfers between devices: 14.2 us -> 23.7 us
    all_to_all x6 -> x4, blocking collectives: 107 us -> 76.9 us  [the longest x1 25.6 us: shards(): lax.all_to_all(logs.reshape(cells, 1, slots), 'row', 0, 0, tiled=True)]
    all_gather x0 -> x1, blocking collectives: none -> 18.4 us  [shards(): lax.all_gather(piece[0], 'col', axis=0, axis_index_groups=groups, tiled=T...]
    ppermute x0 -> x2, starting transfers between devices: none -> 9.69 us  [shards(): other = lax.ppermute(mine, 'col', pairs)]
    pallas_call x9 -> x10, Pallas kernels: 13.3 us -> 13.2 us  [run(): pl.pallas_call(kernel, out_shape=outs, in_specs=[VMEM] * len(args), out_s...]
  transfers between devices with their start and end apart: 1 -> 3, of which waited for: 1 -> 3; matrix products, arithmetic and copies ran while one was open for 0% -> 0% of each run, Pallas kernels for 0% -> 0%
where the time goes in v3:
time: 286 us; the launch traced here: 285 us
  blocking collectives  172 us (60%)
  waiting for transfers between devices  68.2 us (24%)
  starting transfers between devices  23.7 us (8%)
  Pallas kernels  17.6 us (6%)
  local copies, waits for them, and re-layouts  3.06 us (1%)
    all_to_all x2, blocking collectives, shards(): lax.all_to_all(sums.reshape(copies, share, width + LANES), 'col', 0, 0, t...  76.5 us
    all_to_all x1, waiting for transfers between devices, shards(): lax.all_to_all(outgoing.reshape(cells, slots, width), 'row', 0, 0, tiled=...  66.1 us
    all_to_all x1, blocking collectives, shards(): lax.all_to_all(logs.reshape(cells, 1, slots), 'row', 0, 0, tiled=True)  25.6 us
    all_to_all x1, blocking collectives, shards(): logs = lax.all_to_all(logs, 'row', 0, 0, tiled=True).reshape(-1, LANES)  21.9 us
    all_gather x1, blocking collectives, shards(): lax.all_gather(piece[0], 'col', axis=0, axis_index_groups=groups, tiled=T...  18.4 us
    all_to_all x1, blocking collectives, shards(): lax.all_to_all(norms, 'row', 0, 0, tiled=True).reshape(-1, tops * count)  15.3 us
    all_to_all x1, starting transfers between devices, shards(): lax.all_to_all(outgoing.reshape(cells, slots, width), 'row', 0, 0, tiled=...  14 us
    all_to_all x1, blocking collectives, shards(): lax.all_to_all(piece, 'col', 0, 0, axis_index_groups=groups, tiled=True)  14 us
  transfers between devices with their start and end apart: 3, of which 3 were waited for; matrix products, arithmetic and copies ran while one was open for 0% of the time, Pallas kernels for 0%

profile of v3, /device:TPU:1, one launch (start us, length us, event | category | flops | bytes accessed | tf_op | source)
XLA Modules:
  0.0 285.1 jit_solution(4605753639029452687)
XLA Ops:
  0.6 4.4 %pack.1 = bf16[2048,768]{1,0:T(8,128)(2,1)} custom-call(s32[4,32]{1,0:T(4,128)} %bitcast.31, bf16[256,768]{1,0:T(8,128)(2,1)} %bitcast.34), custom_call_target="tpu_custom_call" | custom-call | tf_op jit(solution)/shard_map/pack/pallas_call | solution.py:408
  5.1 14.0 %all-to-all-start = ((bf16[64,32,768]{2,1,0:T(8,128)(2,1)}), bf16[64,32,768]{2,1,0:T(8,128)(2,1)S(1)}, u32[]{:S(2)}, u32[]{:S(2)}) async-start(bf16[64,32,768]{2,1,0:T(8,128)(2,1)} %bitcast.33), calls=%async_computation | async-start | bytes 6291456 | tf_op jit(solution)/shard_map/all_to_all | solution.py:419
  19.3 1.1 copy-done.3
  21.5 66.1 %all-to-all-done = bf16[64,32,768]{2,1,0:T(8,128)(2,1)S(1)} async-done(((bf16[64,32,768]{2,1,0:T(8,128)(2,1)}), bf16[64,32,768]{2,1,0:T(8,128)(2,1)S(1)}, u32[]{:S(2)}, u32[]{:S(2)}) %all-to-all-start) | async-done | bytes 3145760 | tf_op jit(solution)/shard_map/all_to_all | solution.py:419
  87.5 1.0 copy-done.1
  88.6 1.2 stats.1
  89.7 25.6 %all_to_all.35 = f32[64,1,32]{2,1,0:T(1,128)S(1)} all-to-all(f32[64,1,32]{2,1,0:T(1,128)S(1)} %bitcast.29), channel_id=1, replica_groups=mesh['row'=64,'col'=16] {'row'}, dimensions={0} | all-to-all | bytes 16384 | tf_op jit(solution)/shard_map/all_to_all | solution.py:444
  115.4 1.0 norm.1
  116.3 15.3 %all_to_all.36 = f32[64,4,128]{2,1,0:T(4,128)S(1)} all-to-all(f32[64,4,128]{2,1,0:T(4,128)S(1)} %norm.1), channel_id=1, replica_groups=mesh['row'=64,'col'=16] {'row'}, dimensions={0} | all-to-all | bytes 262144 | tf_op jit(solution)/shard_map/all_to_all | solution.py:450
  131.7 2.2 sums.1
  133.9 1.8 index.1
  135.7 55.3 %all_to_all.37.sums_ref = bf16[16,16,896]{2,1,0:T(8,128)(2,1)S(1)} all-to-all(bf16[16,16,896]{2,1,0:T(8,128)(2,1)S(1)} %bitcast.25), channel_id=1, replica_groups=mesh['row'=64,'col'=16] {'col'}, dimensions={0} | all-to-all | bytes 917504 | tf_op jit(solution)/shard_map/all_to_all | solution.py:476
  191.4 18.4 %all-gather = bf16[1,128,896]{2,1,0:T(8,128)(2,1)S(1)} all-gather(bf16[1,16,896]{2,1,0:T(8,128)(2,1)S(1)} %get-tuple-element.25), channel_id=2, replica_groups={{0,2,4,6,8,10,12,14},{1,3,5,7,9,11,13,15},{16,18,20,22,24,26,28,30},{17..., dimensions={1}, use_global_device_ids=true | all-gather | bytes 258048 | tf_op jit(solution)/shard_map/all_gather | solution.py:496
  209.7 7.3 %collective-permute-start = (bf16[128,896]{1,0:T(8,128)(2,1)S(1)}, bf16[128,896]{1,0:T(8,128)(2,1)S(1)}, u32[]{:S(2)}, u32[]{:S(2)}) collective-permute-start(bf16[128,896]{1,0:T(8,128)(2,1)S(1)} %bitcast.22), channel_id=1, source_target_pairs={{0,1},{1,0},{2,3},{3,2},{4,5},{5,4},{6,7},{7,6},{8,9},{9,8},{10,11... | collective-permute-start | bytes 688136 | tf_op jit(solution)/shard_map/ppermute | solution.py:497
  217.0 1.1 collective-permute-done.other_ref
  218.1 1.2 stats_all.1
  219.3 21.9 %all_to_all.38 = f32[64,16,128]{2,1,0:T(8,128)S(1)} all-to-all(f32[64,16,128]{2,1,0:T(8,128)S(1)} %stats_all.1), channel_id=1, replica_groups=mesh['row'=64,'col'=16] {'row'}, dimensions={0} | all-to-all | bytes 1048576 | tf_op jit(solution)/shard_map/all_to_all | solution.py:470
  241.3 3.3 %sums_all.1 = bf16[16,16,896]{2,1,0:T(8,128)(2,1)S(1)} custom-call(bf16[128,896]{1,0:T(8,128)(2,1)S(1)} %bitcast.24, bf16[128,896]{1,0:T(8,128)(2,1)S(1)} %collective-permute-done.other_ref, bf16[2048,768]{1,0:T(8,128)(2,1)S(1)} %bitcast.20, f32[1024,128]{1,0:T(8,128)S(1)} %bitcast.21, bf16[1024,128]{1,0:T(8,128)(2,1)S(1)} %get-tuple-element.26.hot_ref, ...), custom_call_target="tpu_custom_call" | custom-call | tf_op jit(solution)/shard_map/sums_all/pallas_call | solution.py:28
  244.5 21.2 %all_to_all.39.sums_ref = bf16[16,16,896]{2,1,0:T(8,128)(2,1)S(1)} all-to-all(bf16[16,16,896]{2,1,0:T(8,128)(2,1)S(1)} %sums_all.1), channel_id=1, replica_groups=mesh['row'=64,'col'=16] {'col'}, dimensions={0} | all-to-all | bytes 917504 | tf_op jit(solution)/shard_map/all_to_all | solution.py:476
  265.7 0.8 update.3
  266.5 14.0 %all_to_all.40.mine_ref = bf16[8,16,896]{2,1,0:T(8,128)(2,1)S(1)} all-to-all(bf16[8,16,896]{2,1,0:T(8,128)(2,1)S(1)} %get-tuple-element.31), channel_id=1, replica_groups={{0,2,4,6,8,10,12,14},{1,3,5,7,9,11,13,15},{16,18,20,22,24,26,28,30},{17..., dimensions={0} | all-to-all | bytes 458752 | tf_op jit(solution)/shard_map/all_to_all | solution.py:494
  280.5 2.4 collective-permute-start.1
  282.9 1.1 collective-permute-done.1.other_ref
  284.0 1.1 finish.1
  (13 shorter events, 1.5 us)
Async XLA Ops:
  5.1 14.1 %copy-start.5 = (f32[1,256]{1,0:T(1,128)S(1)}, f32[1,256]{1,0:T(1,128)}, u32[]{:S(2)}) copy-start(f32[1,256]{1,0:T(1,128)} %param.7) | copy-start | bytes 3076
  5.1 82.5 %all-to-all-start = ((bf16[64,32,768]{2,1,0:T(8,128)(2,1)}), bf16[64,32,768]{2,1,0:T(8,128)(2,1)S(1)}, u32[]{:S(2)}, u32[]{:S(2)}) async-start(bf16[64,32,768]{2,1,0:T(8,128)(2,1)} %bitcast.33), calls=%async_computation | async-start | bytes 6291456 | tf_op jit(solution)/shard_map/all_to_all | solution.py:419
  19.1 96.2 %copy-start.4 = (s32[1,32,4]{1,2,0:T(4,128)S(1)}, s32[1,32,4]{1,2,0:T(4,128)}, u32[]{:S(2)}) copy-start(s32[1,32,4]{1,2,0:T(4,128)} %param.5) | copy-start | bytes 1540
  19.3 1.1 copy-start.3
  20.7 0.8 copy-start
  87.5 1.0 copy-start.1
  88.5 43.1 %copy-start.2 = (bf16[256,896]{1,0:T(8,128)(2,1)S(1)}, bf16[256,896]{1,0:T(8,128)(2,1)}, u32[]{:S(2)}) copy-start(bf16[256,896]{1,0:T(8,128)(2,1)} %copy-done) | copy-start | bytes 1376260
  209.7 8.4 %collective-permute-start = (bf16[128,896]{1,0:T(8,128)(2,1)S(1)}, bf16[128,896]{1,0:T(8,128)(2,1)S(1)}, u32[]{:S(2)}, u32[]{:S(2)}) collective-permute-start(bf16[128,896]{1,0:T(8,128)(2,1)S(1)} %bitcast.22), channel_id=1, source_target_pairs={{0,1},{1,0},{2,3},{3,2},{4,5},{5,4},{6,7},{7,6},{8,9},{9,8},{10,11... | collective-permute-start | bytes 688136 | tf_op jit(solution)/shard_map/ppermute | solution.py:497
  280.5 3.5 %collective-permute-start.1 = (bf16[8,16,896]{2,1,0:T(8,128)(2,1)S(1)}, bf16[8,16,896]{2,1,0:T(8,128)(2,1)S(1)}, u32[]{:S(2)}, u32[]{:S(2)}) collective-permute-start(bf16[8,16,896]{2,1,0:T(8,128)(2,1)S(1)} %all_to_all.40.mine_ref), channel_id=1, source_target_pairs={{0,1},{1,0},{2,3},{3,2},{4,5},{5,4},{6,7},{7,6},{8,9},{9,8},{10,11... | collective-permute-start | bytes 688136 | tf_op jit(solution)/shard_map/ppermute | solution.py:497

commit v4 on v3

--- a/solution.py
+++ b/solution.py
@@ -9,7 +9,6 @@
 
 STEPS = 2
 LANES = 128
-PARTS = 4
 
 prior_mass = 1.0
 price_rate = 0.5
@@ -39,16 +38,6 @@
 
 def iota(shape, dim):
     return lax.broadcasted_iota(jnp.int32, shape, dim)
-
-
-def exact_dot(a, b, dims):
-    return lax.dot_general(
-        a,
-        b,
-        (dims, ((), ())),
-        precision=lax.Precision.HIGHEST,
-        preferred_element_type=jnp.float32,
-    )
 
 
 def small_dot(a, b, dims):
@@ -100,12 +89,14 @@
         copy.wait()
 
 
-def index_kernel(capacity, per_block, tops, names_ref, hot_ref, mask_ref, empty_ref):
-    total, lanes = names_ref.shape
-    devices = total // PARTS
+def index_kernel(capacity, per_block, tops, held_ref, hot_ref, mask_ref, empty_ref):
+    lanes = held_ref.shape[1]
+    groups = empty_ref.shape[0] * per_block // LANES
+    sent = groups + 2
+    devices = held_ref.shape[0] // sent
     count = lanes // tops
-    cells = names_ref[pl.ds(1, devices, stride=PARTS), :]
-    slots = names_ref[pl.ds(2, devices, stride=PARTS), :]
+    cells = held_ref[pl.ds(groups, devices, stride=sent), :]
+    slots = held_ref[pl.ds(groups + 1, devices, stride=sent), :]
     mine = cells == lax.axis_index("row").astype(jnp.float32)
     to_block = (iota((lanes, count), 0) % count == iota((lanes, count), 1)).astype(jnp.float32)
     to_top = (iota((lanes, tops), 0) // count == iota((lanes, tops), 1)).astype(jnp.float32)
@@ -146,12 +137,6 @@
         empty_ref[g * step : (g + 1) * step, :] = jnp.broadcast_to(1.0 - head, (step, LANES))
 
 
-def pair_place(at, copies):
-    core = lax.axis_index("col") % 2
-    half = copies // 2
-    return 2 * at + core if at < half else 2 * (at - half) + 1 - core
-
-
 def centre_offset(packed, width):
     return (
         packed[:, width : width + 1].astype(jnp.float32)
@@ -173,100 +158,33 @@
     return highest + jnp.log(jnp.sum(jnp.exp(scores - highest), axis=0, keepdims=True))
 
 
-def slot_stats_kernel(chunks, packed_ref, incoming_ref, out_ref):
+def stats_kernel(chunks, cells, packed_ref, incoming_ref, *refs):
+    names_ref, out_ref = refs if len(refs) > 1 else (None, refs[0])
     width = incoming_ref.shape[1]
     packed = packed_ref[...]
     half = packed[:, :width]
     offset = centre_offset(packed, width)
     size = incoming_ref.shape[0] // chunks
-    slots = out_ref.shape[1]
-    part = size // slots
-    for k in range(chunks):
-        logs = row_logs(half, offset, incoming_ref[k * size : (k + 1) * size, :])
-        for o in range(part):
-            out_ref[k * part + o : k * part + o + 1, :] = logs[:, o * slots : (o + 1) * slots]
-
-
-def norm_kernel(per_block, capacity, wanted_ref, back_ref, out_ref):
-    back = back_ref[...]
-    cells = back.shape[0]
-    wanted = wanted_ref[...]
-    hots, _, before = block_names(wanted, cells)
-    tops = len(hots)
-    count = hots[0].shape[1]
-    hot = jnp.concatenate(hots, axis=1)
-    slot = small_dot(
-        hot * jnp.concatenate([before] * tops, axis=1),
-        jnp.ones((cells, capacity * per_block), jnp.float32),
-        ((0,), (0,)),
-    )
-    in_slot = slot == (iota(slot.shape, 1) // per_block).astype(jnp.float32)
-    found = jnp.where(in_slot, exact_dot(hot, back, ((0,), (0,))), 0.0)
-    part = found[:, :per_block]
-    for s in range(1, capacity):
-        part = part + found[:, s * per_block : (s + 1) * per_block]
-    parts = [part[t * count : (t + 1) * count] for t in range(tops)]
-    largest = functools.reduce(jnp.maximum, parts)
-    total = functools.reduce(jnp.add, [jnp.exp(part - largest) for part in parts])
-    norm = largest + jnp.log(total)
-    norm = jnp.concatenate([norm] * capacity, axis=1)
-    norm = jnp.where(in_slot, jnp.concatenate([norm] * tops, axis=0), 0.0)
-    value = exact_dot(hot, norm, ((1,), (0,)))
-    filled = small_dot(hot, in_slot.astype(jnp.float32), ((1,), (0,)))
-    value = jnp.where(filled > 0, value, empty_log)
-    value = jnp.concatenate([value] * (out_ref.shape[2] // value.shape[1]), axis=1)
-    out_ref[:, 0, :] = value
-    names = [wanted[t : t + 1, :].astype(jnp.float32) for t in range(tops)]
-    places = [jnp.sum(one * before, axis=0, keepdims=True) for one in hots]
-    out_ref[:, 1, :] = jnp.broadcast_to(jnp.concatenate(names, axis=1), value.shape)
-    out_ref[:, 2, :] = jnp.broadcast_to(jnp.concatenate(places, axis=1), value.shape)
-    out_ref[:, 3, :] = jnp.zeros(value.shape, jnp.float32)
-
-
-def stats_kernel(chunks, mine_ref, other_ref, incoming_ref, out_ref):
-    width = incoming_ref.shape[1]
-    packed = jnp.concatenate([mine_ref[...], other_ref[...]], axis=0)
-    half = packed[:, :width]
-    offset = centre_offset(packed, width)
-    size = incoming_ref.shape[0] // chunks
     part = size // LANES
+    sent = out_ref.shape[0] // cells
     for k in range(chunks):
         logs = row_logs(half, offset, incoming_ref[k * size : (k + 1) * size, :])
         logs = jnp.concatenate(
             [logs[:, i * LANES : (i + 1) * LANES] for i in range(part)], axis=0
         )
-        for o in range(out_ref.shape[0]):
-            out_ref[o, k * part : (k + 1) * part, :] = logs
-
-
-def slot_sums_kernel(chunks, per_owner, packed_ref, incoming_ref, log_ref, out_ref):
-    width = incoming_ref.shape[1]
-    packed = packed_ref[...]
-    half = packed[:, :width]
-    offset = centre_offset(packed, width)
-    centres = packed.shape[0]
-    size = incoming_ref.shape[0] // chunks
-    part = size // per_owner
-    total = jnp.zeros((centres, width), jnp.float32)
-    load = jnp.zeros((centres, 1), jnp.float32)
-    for k in range(chunks):
-        rows = incoming_ref[k * size : (k + 1) * size, :]
-        places = [(k * part + o) * PARTS for o in range(part)]
-        logs = jnp.concatenate([log_ref[p : p + 1, :per_owner] for p in places], axis=1)
-        weight = jnp.exp(score_chunk(half, offset, rows) - logs)
-        load = load + jnp.sum(weight, axis=1, keepdims=True)
-        total = total + jnp.dot(
-            weight.astype(jnp.bfloat16), rows, preferred_element_type=jnp.float32
-        )
-    out_ref[...] = packed_with(total, load)
+        for o in range(cells):
+            out_ref[o * sent + k * part : o * sent + (k + 1) * part, :] = logs
+    if names_ref is not None:
+        for o in range(cells):
+            out_ref[(o + 1) * sent - 2 : (o + 1) * sent, :] = names_ref[...]
 
 
 def sums_kernel(
     chunks,
     tops,
     per_block,
-    mine_ref,
-    other_ref,
+    cells,
+    packed_ref,
     incoming_ref,
     logs_ref,
     hot_ref,
@@ -275,18 +193,18 @@
     out_ref,
 ):
     width = incoming_ref.shape[1]
-    packed = jnp.concatenate([mine_ref[...], other_ref[...]], axis=0)
+    packed = packed_ref[...]
     half = packed[:, :width]
     offset = centre_offset(packed, width)
     centres = packed.shape[0]
     size = incoming_ref.shape[0] // chunks
     part = size // LANES
     groups = incoming_ref.shape[0] // LANES
-    cells = logs_ref.shape[0] // groups
+    sent = logs_ref.shape[0] // cells
     step = empty_ref.shape[0] // groups
 
     def group_logs(g):
-        logs = logs_ref[pl.ds(g, cells, stride=groups), :]
+        logs = logs_ref[pl.ds(g, cells, stride=sent), :]
         high = logs.astype(jnp.bfloat16)
         rest = logs - high.astype(jnp.float32)
         middle = rest.astype(jnp.bfloat16)
@@ -321,10 +239,7 @@
         total = total + jnp.dot(
             weight.astype(jnp.bfloat16), rows, preferred_element_type=jnp.float32
         )
-    full = packed_with(total, load)
-    share = out_ref.shape[1]
-    for at in range(out_ref.shape[0]):
-        out_ref[pair_place(at, out_ref.shape[0])] = full[at * share : (at + 1) * share]
+    out_ref[...] = packed_with(total, load)
 
 
 def packed_with(means, column):
@@ -346,7 +261,7 @@
     return jnp.concatenate([means.astype(jnp.bfloat16), tail.astype(jnp.bfloat16)], axis=1)
 
 
-def start_kernel(means_ref, price_ref, packed_ref, own_ref, cost_ref):
+def start_kernel(cells, wanted_ref, means_ref, price_ref, packed_ref, own_ref, cost_ref, names_ref):
     means = means_ref[...]
     offset = 0.5 * jnp.sum(means * means, axis=1, keepdims=True) + price_ref[...]
     packed_ref[...] = packed_with(means, offset)
@@ -354,6 +269,12 @@
     place = pl.multiple_of(lax.axis_index("col") * share, share)
     own_ref[...] = means_ref[pl.ds(place, share), :]
     cost_ref[...] = price_ref[pl.ds(place, share), :]
+    wanted = wanted_ref[...]
+    hots, _, before = block_names(wanted, cells)
+    names = [wanted[t : t + 1, :].astype(jnp.float32) for t in range(len(hots))]
+    places = [jnp.sum(hot * before, axis=0, keepdims=True) for hot in hots]
+    names_ref[0:1, :] = jnp.concatenate(names, axis=1)
+    names_ref[1:2, :] = jnp.concatenate(places, axis=1)
 
 
 def update_kernel(target, last, sums_ref, means_ref, price_ref, packed_ref, new_ref, cost_ref):
@@ -371,22 +292,14 @@
         packed_ref[copy] = packed
 
 
-def finish_kernel(mine_ref, other_ref, means_ref, price_ref):
+def finish_kernel(packed_ref, means_ref, price_ref):
     width = means_ref.shape[1]
-    half, share = mine_ref.shape[:2]
-    swapped = lax.axis_index("col") % 2 > 0
-    for z in range(half):
-        mine, other = mine_ref[z].astype(jnp.float32), other_ref[z].astype(jnp.float32)
-        for at, part in enumerate(
-            (jnp.where(swapped, other, mine), jnp.where(swapped, mine, other))
-        ):
-            first = (2 * z + at) * share
-            means_ref[first : first + share, :] = part[:, :width]
-            price = part[:, width : width + 1] + part[:, width + 1 : width + 2]
-            price = price + part[:, width + 2 : width + 3]
-            here = iota((share, share), 0) == iota((share, share), 1)
-            price = jnp.sum(jnp.where(here, price, 0.0), axis=0, keepdims=True)
-            price_ref[:, first : first + share] = price
+    packed = packed_ref[...]
+    means_ref[...] = packed[:, :width].astype(jnp.float32)
+    price = centre_offset(packed, width)
+    count = packed.shape[0]
+    here = iota((count, count), 0) == iota((count, count), 1)
+    price_ref[...] = jnp.sum(jnp.where(here, price, 0.0), axis=0, keepdims=True)
 
 
 def shards(points, candidates, centroids, prices):
@@ -420,81 +333,62 @@
     incoming = incoming.reshape(rows, width)
 
     price_column = prices[0].reshape(centres, 1)
-    packed, means, price = on_chip(
-        start_kernel,
+    packed, means, price, names = on_chip(
+        functools.partial(start_kernel, cells),
         "start",
         (
             jax.ShapeDtypeStruct((centres, width + LANES), jnp.bfloat16),
             jax.ShapeDtypeStruct((share, width), jnp.float32),
             jax.ShapeDtypeStruct((share, 1), jnp.float32),
+            jax.ShapeDtypeStruct((2, tops * count), jnp.float32),
         ),
-        (False, False),
-    )(centroids[0], price_column)
-
-    sums_shape = jax.ShapeDtypeStruct((centres, width + LANES), jnp.bfloat16)
+        (False, False, False),
+    )(wanted, centroids[0], price_column)
+
+    groups = rows // LANES
     for sweep_index in range(STEPS):
         last = sweep_index == STEPS - 1
-        if sweep_index == 0:
-            logs = on_chip(
-                functools.partial(slot_stats_kernel, chunks),
-                "stats",
-                jax.ShapeDtypeStruct((cells, slots), jnp.float32),
-                (False, True),
-            )(packed, incoming)
-            logs = lax.all_to_all(logs.reshape(cells, 1, slots), "row", 0, 0, tiled=True)
-            norms = on_chip(
-                functools.partial(norm_kernel, per_block, capacity),
-                "norm",
-                jax.ShapeDtypeStruct((cells, PARTS, tops * count), jnp.float32),
-            )(wanted, logs.reshape(cells, slots))
-            norms = lax.all_to_all(norms, "row", 0, 0, tiled=True).reshape(-1, tops * count)
-            sums = on_chip(
-                functools.partial(slot_sums_kernel, chunks, slots), "sums", sums_shape, (False, True, True)
-            )(packed, incoming, norms)
+        first = sweep_index == 0
+        sent = groups + 2 if first else groups
+        logs = on_chip(
+            functools.partial(stats_kernel, chunks, cells),
+            "stats",
+            jax.ShapeDtypeStruct((cells * sent, LANES), jnp.float32),
+            (False, True, False) if first else None,
+        )(packed, incoming, *((names,) if first else ()))
+        logs = logs.reshape(cells, sent // 2, 2, LANES)
+        logs = lax.all_to_all(logs, "row", 0, 0, tiled=True).reshape(cells * sent, LANES)
+        if first:
+            lines = rows // per_block
             hot, mask, empty = on_chip(
                 functools.partial(index_kernel, capacity, per_block, tops),
                 "index",
                 (
-                    jax.ShapeDtypeStruct((rows // per_block * tops, LANES), jnp.bfloat16),
-                    jax.ShapeDtypeStruct((rows // per_block * tops, LANES), jnp.bfloat16),
-                    jax.ShapeDtypeStruct((rows // per_block, LANES), jnp.float32),
+                    jax.ShapeDtypeStruct((lines * tops, LANES), jnp.bfloat16),
+                    jax.ShapeDtypeStruct((lines * tops, LANES), jnp.bfloat16),
+                    jax.ShapeDtypeStruct((lines, LANES), jnp.float32),
                 ),
-            )(norms)
-            sums, hot, mask, empty = lax.optimization_barrier((sums, hot, mask, empty))
-        else:
-            logs = on_chip(
-                functools.partial(stats_kernel, chunks),
-                "stats_all",
-                jax.ShapeDtypeStruct((cells, rows // LANES, LANES), jnp.float32),
-            )(mine, other, incoming)
-            logs = lax.all_to_all(logs, "row", 0, 0, tiled=True).reshape(-1, LANES)
-            sums = on_chip(
-                functools.partial(sums_kernel, chunks, tops, per_block),
-                "sums_all",
-                jax.ShapeDtypeStruct((copies, share, width + LANES), jnp.bfloat16),
-            )(mine, other, incoming, logs, hot, mask, empty)
+            )(logs)
+        sums = on_chip(
+            functools.partial(sums_kernel, chunks, tops, per_block, cells),
+            "sums",
+            jax.ShapeDtypeStruct((centres, width + LANES), jnp.bfloat16),
+            (False,) + (True,) * 5 if first else None,
+        )(packed, incoming, logs, hot, mask, empty)
         pieces = lax.all_to_all(
             sums.reshape(copies, share, width + LANES), "col", 0, 0, tiled=True
         )
-        half = copies // 2
-        piece_shape = (half if last else 1, share, width + LANES)
         piece, means, price = on_chip(
             functools.partial(update_kernel, target, last),
             "update",
             (
-                jax.ShapeDtypeStruct(piece_shape, jnp.bfloat16),
+                jax.ShapeDtypeStruct((copies, share, width + LANES), jnp.bfloat16),
                 jax.ShapeDtypeStruct((share, width), jnp.float32),
                 jax.ShapeDtypeStruct((share, 1), jnp.float32),
             ),
             (True, False, False),
         )(pieces, means, price)
-        groups = [list(range(0, copies, 2)), list(range(1, copies, 2))]
-        pairs = [(i, i ^ 1) for i in range(copies)]
-        if last:
-            mine = lax.all_to_all(piece, "col", 0, 0, axis_index_groups=groups, tiled=True)
-        else:
-            mine = lax.all_gather(piece[0], "col", axis=0, axis_index_groups=groups, tiled=True)
-        other = lax.ppermute(mine, "col", pairs)
+        packed = lax.all_to_all(piece, "col", 0, 0, tiled=True).reshape(centres, width + LANES)
 
     new_centroids, new_prices = on_chip(
         finish_kernel,
@@ -503,7 +397,7 @@
             jax.ShapeDtypeStruct((centres, width), jnp.float32),
             jax.ShapeDtypeStruct((1, centres), jnp.float32),
         ),
-    )(mine, other)
+    )(packed)
     return (new_centroids[None], new_prices)
 
 

time: 286 us -> 270 us (0.944)
  starting transfers between devices: 23.7 us -> 14 us
  blocking collectives: 172 us -> 168 us
    all_gather x1 -> x0, blocking collectives: 18.4 us -> none  [shards(): lax.all_gather(piece[0], 'col', axis=0, axis_index_groups=groups, tiled=T...]
    all_to_all x4, blocking collectives: 76.9 us -> 90.8 us  [the longest x2 53.6 us: shards(): lax.all_to_all(logs, 'row', 0, 0, tiled=True).reshape(cells * sent, LANES)]
    ppermute x2 -> x0, starting transfers between devices: 9.69 us -> none  [shards(): other = lax.ppermute(mine, 'col', pairs)]
    pallas_call x10 -> x9, Pallas kernels: 13.2 us -> 13.2 us  [run(): pl.pallas_call(kernel, out_shape=outs, in_specs=[VMEM] * len(args), out_s...]
  transfers between devices with their start and end apart: 3 -> 1, of which waited for: 3 -> 1; matrix products, arithmetic and copies ran while one was open for 0% -> 0% of each run, Pallas kernels for 0% -> 0%
where the time goes in v4:
time: 270 us
  blocking collectives  168 us (62%)
  waiting for transfers between devices  66 us (24%)
  Pallas kernels  17.6 us (7%)
  starting transfers between devices  14 us (5%)
  local copies, waits for them, and re-layouts  3.05 us (1%)
    all_to_all x2, blocking collectives, shards(): lax.all_to_all(sums.reshape(copies, share, width + LANES), 'col', 0, 0, t...  77.4 us
    all_to_all x1, waiting for transfers between devices, shards(): lax.all_to_all(outgoing.reshape(cells, slots, width), 'row', 0, 0, tiled=...  66 us
    all_to_all x2, blocking collectives, shards(): lax.all_to_all(logs, 'row', 0, 0, tiled=True).reshape(cells * sent, LANES)  53.6 us
    all_to_all x2, blocking collectives, shards(): lax.all_to_all(piece, 'col', 0, 0, tiled=True)  37.1 us
    all_to_all x1, starting transfers between devices, shards(): lax.all_to_all(outgoing.reshape(cells, slots, width), 'row', 0, 0, tiled=...  14 us
    pallas_call x9, Pallas kernels, run(): pl.pallas_call(kernel, out_shape=outs, in_specs=[VMEM] * len(args), out_s...  13.2 us
  transfers between devices with their start and end apart: 1, of which 1 were waited for; matrix products, arithmetic and copies ran while one was open for 0% of the time, Pallas kernels for 0%

profile of v4, /device:TPU:1, one launch (start us, length us, event | category | flops | bytes accessed | tf_op | source)
XLA Modules:
  0.0 269.7 jit_solution(6360438926111901674)
XLA Ops:
  0.6 4.4 %pack.1 = bf16[2048,768]{1,0:T(8,128)(2,1)} custom-call(s32[4,32]{1,0:T(4,128)} %bitcast.32, bf16[256,768]{1,0:T(8,128)(2,1)} %bitcast.35), custom_call_target="tpu_custom_call" | custom-call | tf_op jit(solution)/shard_map/pack/pallas_call | solution.py:321
  5.1 0.0 copy-start.4
  5.1 14.0 %all-to-all-start = ((bf16[64,32,768]{2,1,0:T(8,128)(2,1)}), bf16[64,32,768]{2,1,0:T(8,128)(2,1)S(1)}, u32[]{:S(2)}, u32[]{:S(2)}) async-start(bf16[64,32,768]{2,1,0:T(8,128)(2,1)} %bitcast.34), calls=%async_computation | async-start | bytes 6291456 | tf_op jit(solution)/shard_map/all_to_all | solution.py:332
  19.1 0.1 copy.6.price_ref
  19.3 1.1 copy-done.2
  20.4 0.3 start.1
  20.7 0.0 copy-start
  20.7 0.8 copy-done
  21.5 66.0 %all-to-all-done = bf16[64,32,768]{2,1,0:T(8,128)(2,1)S(1)} async-done(((bf16[64,32,768]{2,1,0:T(8,128)(2,1)}), bf16[64,32,768]{2,1,0:T(8,128)(2,1)S(1)}, u32[]{:S(2)}, u32[]{:S(2)}) %all-to-all-start) | async-done | bytes 3145760 | tf_op jit(solution)/shard_map/all_to_all | solution.py:332
  87.5 1.0 copy-done.1
  88.6 1.2 stats.2
  89.7 30.3 %all_to_all.35 = f32[64,9,2,128]{3,2,1,0:T(2,128)S(1)} all-to-all(f32[64,9,2,128]{3,2,1,0:T(2,128)S(1)} %bitcast.25), channel_id=1, replica_groups=mesh['row'=64,'col'=16] {'row'}, dimensions={0} | all-to-all | bytes 1179648 | tf_op jit(solution)/shard_map/all_to_all | solution.py:360
  120.0 1.8 index.1
  121.9 3.2 %sums.2 = bf16[256,896]{1,0:T(8,128)(2,1)S(1)} custom-call(bf16[256,896]{1,0:T(8,128)(2,1)S(1)} %copy-done.1, bf16[2048,768]{1,0:T(8,128)(2,1)S(1)} %bitcast.18, f32[1152,128]{1,0:T(8,128)S(1)} %bitcast.22, bf16[1024,128]{1,0:T(8,128)(2,1)S(1)} %get-tuple-element.17.hot_ref, bf16[1024,128]{1,0:T(8,128)(2,1)S(1)} %get-tuple-element.18.mask_ref, ...), custom_call_target="tpu_custom_call" | custom-call | tf_op jit(solution)/shard_map/sums/pallas_call | solution.py:27
  125.1 57.2 %all_to_all.36.sums_ref = bf16[16,16,896]{2,1,0:T(8,128)(2,1)S(1)} all-to-all(bf16[16,16,896]{2,1,0:T(8,128)(2,1)S(1)} %bitcast.30), channel_id=1, replica_groups=mesh['row'=64,'col'=16] {'col'}, dimensions={0} | all-to-all | bytes 917504 | tf_op jit(solution)/shard_map/all_to_all | solution.py:378
  182.3 0.3 update.2
  182.6 18.6 %all_to_all.37 = bf16[16,16,896]{2,1,0:T(8,128)(2,1)S(1)} all-to-all(bf16[16,16,896]{2,1,0:T(8,128)(2,1)S(1)} %get-tuple-element.22), channel_id=1, replica_groups=mesh['row'=64,'col'=16] {'col'}, dimensions={0} | all-to-all | bytes 917504 | tf_op jit(solution)/shard_map/all_to_all | solution.py:391
  201.2 1.2 stats.3
  202.4 23.4 %all_to_all.38 = f32[64,8,2,128]{3,2,1,0:T(2,128)S(1)} all-to-all(f32[64,8,2,128]{3,2,1,0:T(2,128)S(1)} %bitcast.27), channel_id=1, replica_groups=mesh['row'=64,'col'=16] {'row'}, dimensions={0} | all-to-all | bytes 1048576 | tf_op jit(solution)/shard_map/all_to_all | solution.py:360
  225.8 3.3 %sums.3 = bf16[256,896]{1,0:T(8,128)(2,1)S(1)} custom-call(bf16[256,896]{1,0:T(8,128)(2,1)S(1)} %bitcast.24, bf16[2048,768]{1,0:T(8,128)(2,1)S(1)} %bitcast.20, f32[1024,128]{1,0:T(8,128)S(1)} %bitcast.26, bf16[1024,128]{1,0:T(8,128)(2,1)S(1)} %get-tuple-element.17.hot_ref, bf16[1024,128]{1,0:T(8,128)(2,1)S(1)} %get-tuple-element.18.mask_ref, ...), custom_call_target="tpu_custom_call" | custom-call | tf_op jit(solution)/shard_map/sums/pallas_call | solution.py:27
  229.1 20.2 %all_to_all.39.sums_ref = bf16[16,16,896]{2,1,0:T(8,128)(2,1)S(1)} all-to-all(bf16[16,16,896]{2,1,0:T(8,128)(2,1)S(1)} %bitcast.28), channel_id=1, replica_groups=mesh['row'=64,'col'=16] {'col'}, dimensions={0} | all-to-all | bytes 917504 | tf_op jit(solution)/shard_map/all_to_all | solution.py:378
  249.3 0.8 update.3
  250.1 18.6 %all_to_all.40 = bf16[16,16,896]{2,1,0:T(8,128)(2,1)S(1)} all-to-all(bf16[16,16,896]{2,1,0:T(8,128)(2,1)S(1)} %get-tuple-element.25), channel_id=1, replica_groups=mesh['row'=64,'col'=16] {'col'}, dimensions={0} | all-to-all | bytes 917504 | tf_op jit(solution)/shard_map/all_to_all | solution.py:391
  268.7 1.0 finish.1
  (5 shorter events, 0.0 us)
Async XLA Ops:
  5.1 14.1 %copy-start.4 = (f32[1,256]{1,0:T(1,128)S(1)}, f32[1,256]{1,0:T(1,128)}, u32[]{:S(2)}) copy-start(f32[1,256]{1,0:T(1,128)} %param.7) | copy-start | bytes 3076
  5.1 14.2 %copy-start.3 = (s32[1,32,4]{1,2,0:T(4,128)S(1)}, s32[1,32,4]{1,2,0:T(4,128)}, u32[]{:S(2)}) copy-start(s32[1,32,4]{1,2,0:T(4,128)} %param.5) | copy-start | bytes 1540
  5.1 82.5 %all-to-all-start = ((bf16[64,32,768]{2,1,0:T(8,128)(2,1)}), bf16[64,32,768]{2,1,0:T(8,128)(2,1)S(1)}, u32[]{:S(2)}, u32[]{:S(2)}) async-start(bf16[64,32,768]{2,1,0:T(8,128)(2,1)} %bitcast.34), calls=%async_computation | async-start | bytes 6291456 | tf_op jit(solution)/shard_map/all_to_all | solution.py:332
  19.3 1.1 copy-start.2
  20.7 0.8 copy-start
  87.5 1.0 copy-start.1

commit v5 on v4

--- a/solution.py
+++ b/solution.py
@@ -9,6 +9,7 @@
 
 STEPS = 2
 LANES = 128
+EXTRA = 8
 
 prior_mass = 1.0
 price_rate = 0.5
@@ -137,12 +138,58 @@
         empty_ref[g * step : (g + 1) * step, :] = jnp.broadcast_to(1.0 - head, (step, LANES))
 
 
-def centre_offset(packed, width):
-    return (
-        packed[:, width : width + 1].astype(jnp.float32)
-        + packed[:, width + 1 : width + 2].astype(jnp.float32)
-        + packed[:, width + 2 : width + 3].astype(jnp.float32)
-    )
+def share_rows(share, width):
+    return width // LANES * share + EXTRA
+
+
+def store_share(ref, first, means, column):
+    share, width = means.shape
+    for tile in range(width // LANES):
+        at = first + tile * share
+        ref[at : at + share, :] = means[:, tile * LANES : (tile + 1) * LANES].astype(jnp.bfloat16)
+    line = jnp.sum(
+        jnp.where(iota((share, LANES), 0) == iota((share, LANES), 1), column, 0.0),
+        axis=0,
+        keepdims=True,
+    )
+    high = line.astype(jnp.bfloat16).astype(jnp.float32)
+    middle = (line - high).astype(jnp.bfloat16).astype(jnp.float32)
+    low = line - high - middle
+    row = iota((EXTRA, LANES), 0)
+    tail = jnp.where(
+        row == 0, high, jnp.where(row == 1, middle, jnp.where(row == 2, low, 0.0))
+    )
+    at = first + width // LANES * share
+    ref[at : at + EXTRA, :] = tail.astype(jnp.bfloat16)
+
+
+def load_column(tail, share):
+    line = tail[0:1, :] + tail[1:2, :] + tail[2:3, :]
+    here = iota((share, LANES), 0) == iota((share, LANES), 1)
+    return jnp.sum(jnp.where(here, line, 0.0), axis=1, keepdims=True)
+
+
+def load_shares(ref, share, width):
+    tiles = width // LANES
+    size = share_rows(share, width)
+    firsts = [o * size for o in range(ref.shape[0] // size)]
+    means = jnp.concatenate(
+        [
+            jnp.concatenate(
+                [ref[f + t * share : f + (t + 1) * share, :] for f in firsts], axis=0
+            )
+            for t in range(tiles)
+        ],
+        axis=1,
+    )
+    column = jnp.concatenate(
+        [
+            load_column(ref[f + size - EXTRA : f + size, :].astype(jnp.float32), share)
+            for f in firsts
+        ],
+        axis=0,
+    )
+    return means, column
 
 
 def score_chunk(half, offset, rows):
@@ -158,12 +205,10 @@
     return highest + jnp.log(jnp.sum(jnp.exp(scores - highest), axis=0, keepdims=True))
 
 
-def stats_kernel(chunks, cells, packed_ref, incoming_ref, *refs):
+def stats_kernel(chunks, cells, share, packed_ref, incoming_ref, *refs):
     names_ref, out_ref = refs if len(refs) > 1 else (None, refs[0])
     width = incoming_ref.shape[1]
-    packed = packed_ref[...]
-    half = packed[:, :width]
-    offset = centre_offset(packed, width)
+    half, offset = load_shares(packed_ref, share, width)
     size = incoming_ref.shape[0] // chunks
     part = size // LANES
     sent = out_ref.shape[0] // cells
@@ -184,6 +229,7 @@
     tops,
     per_block,
     cells,
+    share,
     packed_ref,
     incoming_ref,
     logs_ref,
@@ -193,10 +239,8 @@
     out_ref,
 ):
     width = incoming_ref.shape[1]
-    packed = packed_ref[...]
-    half = packed[:, :width]
-    offset = centre_offset(packed, width)
-    centres = packed.shape[0]
+    half, offset = load_shares(packed_ref, share, width)
+    centres = half.shape[0]
     size = incoming_ref.shape[0] // chunks
     part = size // LANES
     groups = incoming_ref.shape[0] // LANES
@@ -239,33 +283,18 @@
         total = total + jnp.dot(
             weight.astype(jnp.bfloat16), rows, preferred_element_type=jnp.float32
         )
-    out_ref[...] = packed_with(total, load)
-
-
-def packed_with(means, column):
-    high = column.astype(jnp.bfloat16)
-    rest = column - high.astype(jnp.float32)
-    middle = rest.astype(jnp.bfloat16)
-    low = (rest - middle.astype(jnp.float32)).astype(jnp.bfloat16)
-    lane = iota((means.shape[0], LANES), 1)
-    zero = jnp.zeros((means.shape[0], LANES), jnp.bfloat16).astype(jnp.float32)
-    tail = jnp.where(
-        lane == 0,
-        high.astype(jnp.float32),
-        jnp.where(
-            lane == 1,
-            middle.astype(jnp.float32),
-            jnp.where(lane == 2, low.astype(jnp.float32), zero),
-        ),
-    )
-    return jnp.concatenate([means.astype(jnp.bfloat16), tail.astype(jnp.bfloat16)], axis=1)
+    for o in range(centres // share):
+        here = slice(o * share, (o + 1) * share)
+        store_share(out_ref, o * share_rows(share, width), total[here], load[here])
 
 
 def start_kernel(cells, wanted_ref, means_ref, price_ref, packed_ref, own_ref, cost_ref, names_ref):
     means = means_ref[...]
     offset = 0.5 * jnp.sum(means * means, axis=1, keepdims=True) + price_ref[...]
-    packed_ref[...] = packed_with(means, offset)
-    share = own_ref.shape[0]
+    share, width = own_ref.shape
+    for o in range(means.shape[0] // share):
+        here = slice(o * share, (o + 1) * share)
+        store_share(packed_ref, o * share_rows(share, width), means[here], offset[here])
     place = pl.multiple_of(lax.axis_index("col") * share, share)
     own_ref[...] = means_ref[pl.ds(place, share), :]
     cost_ref[...] = price_ref[pl.ds(place, share), :]
@@ -278,26 +307,30 @@
 
 
 def update_kernel(target, last, sums_ref, means_ref, price_ref, packed_ref, new_ref, cost_ref):
-    width = means_ref.shape[1]
-    sums = sums_ref[...].astype(jnp.float32)
-    total = jnp.sum(sums, axis=0)
-    load = total[:, width : width + 1] + total[:, width + 1 : width + 2] + total[:, width + 2 : width + 3]
-    means = (total[:, :width] + prior_mass * means_ref[...]) / (load + prior_mass)
+    share, width = means_ref.shape
+    size = share_rows(share, width)
+    copies = sums_ref.shape[0] // size
+    total = sums_ref[0:size, :].astype(jnp.float32)
+    for copy in range(1, copies):
+        total = total + sums_ref[copy * size : (copy + 1) * size, :].astype(jnp.float32)
+    load = load_column(total[size - EXTRA :], share)
+    tiles = [total[t * share : (t + 1) * share] for t in range(width // LANES)]
+    total = jnp.concatenate(tiles, axis=1)
+    means = (total + prior_mass * means_ref[...]) / (load + prior_mass)
     price = price_ref[...] + price_rate * jnp.log((load + prior_mass) / (target + prior_mass))
     new_ref[...] = means
     cost_ref[...] = price
     column = price if last else 0.5 * jnp.sum(means * means, axis=1, keepdims=True) + price
-    packed = packed_with(means, column)
-    for copy in range(packed_ref.shape[0]):
-        packed_ref[copy] = packed
-
-
-def finish_kernel(packed_ref, means_ref, price_ref):
-    width = means_ref.shape[1]
-    packed = packed_ref[...]
-    means_ref[...] = packed[:, :width].astype(jnp.float32)
-    price = centre_offset(packed, width)
-    count = packed.shape[0]
+    store_share(packed_ref, 0, means, column)
+    packed = packed_ref[0:size, :]
+    for copy in range(1, copies):
+        packed_ref[copy * size : (copy + 1) * size, :] = packed
+
+
+def finish_kernel(share, packed_ref, means_ref, price_ref):
+    means, price = load_shares(packed_ref, share, means_ref.shape[1])
+    means_ref[...] = means.astype(jnp.float32)
+    count = means.shape[0]
     here = iota((count, count), 0) == iota((count, count), 1)
     price_ref[...] = jnp.sum(jnp.where(here, price, 0.0), axis=0, keepdims=True)
 
@@ -316,6 +349,8 @@
     share = centres // copies
     target = copies * count * per_block / centres
     chunks = 4
+    size = share_rows(share, width)
+    packed_shape = jax.ShapeDtypeStruct((copies * size, LANES), jnp.bfloat16)
 
     chunk = rows // chunks
     outgoing = pl.pallas_call(
@@ -337,7 +372,7 @@
         functools.partial(start_kernel, cells),
         "start",
         (
-            jax.ShapeDtypeStruct((centres, width + LANES), jnp.bfloat16),
+            packed_shape,
             jax.ShapeDtypeStruct((share, width), jnp.float32),
             jax.ShapeDtypeStruct((share, 1), jnp.float32),
             jax.ShapeDtypeStruct((2, tops * count), jnp.float32),
@@ -351,7 +386,7 @@
         first = sweep_index == 0
         sent = groups + 2 if first else groups
         logs = on_chip(
-            functools.partial(stats_kernel, chunks, cells),
+            functools.partial(stats_kernel, chunks, cells, share),
             "stats",
             jax.ShapeDtypeStruct((cells * sent, LANES), jnp.float32),
             (False, True, False) if first else None,
@@ -370,28 +405,27 @@
                 ),
             )(logs)
         sums = on_chip(
-            functools.partial(sums_kernel, chunks, tops, per_block, cells),
+            functools.partial(sums_kernel, chunks, tops, per_block, cells, share),
             "sums",
-            jax.ShapeDtypeStruct((centres, width + LANES), jnp.bfloat16),
+            packed_shape,
             (False,) + (True,) * 5 if first else None,
         )(packed, incoming, logs, hot, mask, empty)
-        pieces = lax.all_to_all(
-            sums.reshape(copies, share, width + LANES), "col", 0, 0, tiled=True
-        )
+        pieces = lax.all_to_all(sums.reshape(copies, size, LANES), "col", 0, 0, tiled=True)
         piece, means, price = on_chip(
             functools.partial(update_kernel, target, last),
             "update",
             (
-                jax.ShapeDtypeStruct((copies, share, width + LANES), jnp.bfloat16),
+                packed_shape,
                 jax.ShapeDtypeStruct((share, width), jnp.float32),
                 jax.ShapeDtypeStruct((share, 1), jnp.float32),
             ),
             (True, False, False),
-        )(pieces, means, price)
-        packed = lax.all_to_all(piece, "col", 0, 0, tiled=True).reshape(centres, width + LANES)
+        )(pieces.reshape(copies * size, LANES), means, price)
+        packed = lax.all_to_all(piece.reshape(copies, size, LANES), "col", 0, 0, tiled=True)
+        packed = packed.reshape(copies * size, LANES)
 
     new_centroids, new_prices = on_chip(
-        finish_kernel,
+        functools.partial(finish_kernel, share),
         "finish",
         (
             jax.ShapeDtypeStruct((centres, width), jnp.float32),

time: 270 us -> 268 us (level)
  blocking collectives: 168 us -> 165 us
    all_to_all x4, blocking collectives: 115 us -> 112 us  [the longest x2 75.9 us: shards(): lax.all_to_all(sums.reshape(copies, size, LANES), 'col', 0, 0, tiled=True)]
where the time goes in v5:
time: 268 us; the launch traced here: 267 us
  blocking collectives  165 us (62%)
  waiting for transfers between devices  66.1 us (25%)
  Pallas kernels  17.6 us (7%)
  starting transfers between devices  14 us (5%)
  local copies, waits for them, and re-layouts  3.03 us (1%)
    all_to_all x2, blocking collectives, shards(): lax.all_to_all(sums.reshape(copies, size, LANES), 'col', 0, 0, tiled=True)  75.9 us
    all_to_all x1, waiting for transfers between devices, shards(): lax.all_to_all(outgoing.reshape(cells, slots, width), 'row', 0, 0, tiled=...  66.1 us
    all_to_all x2, blocking collectives, shards(): lax.all_to_all(logs, 'row', 0, 0, tiled=True).reshape(cells * sent, LANES)  53.8 us
    all_to_all x2, blocking collectives, shards(): lax.all_to_all(piece.reshape(copies, size, LANES), 'col', 0, 0, tiled=True)  35.7 us
    all_to_all x1, starting transfers between devices, shards(): lax.all_to_all(outgoing.reshape(cells, slots, width), 'row', 0, 0, tiled=...  14 us
    pallas_call x9, Pallas kernels, run(): pl.pallas_call(kernel, out_shape=outs, in_specs=[VMEM] * len(args), out_s...  13.2 us
  transfers between devices with their start and end apart: 1, of which 1 were waited for; matrix products, arithmetic and copies ran while one was open for 0% of the time, Pallas kernels for 0%

profile of v5, /device:TPU:1, one launch (start us, length us, event | category | flops | bytes accessed | tf_op | source)
XLA Modules:
  0.0 267.0 jit_solution(1612060785411317875)
XLA Ops:
  0.6 4.4 %pack.1 = bf16[2048,768]{1,0:T(8,128)(2,1)} custom-call(s32[4,32]{1,0:T(4,128)} %bitcast.40, bf16[256,768]{1,0:T(8,128)(2,1)} %bitcast.43), custom_call_target="tpu_custom_call" | custom-call | tf_op jit(solution)/shard_map/pack/pallas_call | solution.py:356
  5.1 0.0 copy-start.4
  5.1 14.0 %all-to-all-start = ((bf16[64,32,768]{2,1,0:T(8,128)(2,1)}), bf16[64,32,768]{2,1,0:T(8,128)(2,1)S(1)}, u32[]{:S(2)}, u32[]{:S(2)}) async-start(bf16[64,32,768]{2,1,0:T(8,128)(2,1)} %bitcast.42), calls=%async_computation | async-start | bytes 6291456 | tf_op jit(solution)/shard_map/all_to_all | solution.py:367
  19.1 0.1 copy.6.price_ref
  19.3 0.0 copy-start.2
  19.3 1.1 copy-done.2
  20.4 0.3 start.1
  20.7 0.7 copy-done
  21.5 66.1 %all-to-all-done = bf16[64,32,768]{2,1,0:T(8,128)(2,1)S(1)} async-done(((bf16[64,32,768]{2,1,0:T(8,128)(2,1)}), bf16[64,32,768]{2,1,0:T(8,128)(2,1)S(1)}, u32[]{:S(2)}, u32[]{:S(2)}) %all-to-all-start) | async-done | bytes 3145760 | tf_op jit(solution)/shard_map/all_to_all | solution.py:367
  87.5 1.0 copy-done.1
  88.5 1.2 stats.2
  89.7 30.3 %all_to_all.35 = f32[64,9,2,128]{3,2,1,0:T(2,128)S(1)} all-to-all(f32[64,9,2,128]{3,2,1,0:T(2,128)S(1)} %bitcast.29), channel_id=1, replica_groups=mesh['row'=64,'col'=16] {'row'}, dimensions={0} | all-to-all | bytes 1179648 | tf_op jit(solution)/shard_map/all_to_all | solution.py:395
  120.0 1.8 index.1
  121.9 3.3 %sums.2 = bf16[1664,128]{1,0:T(8,128)(2,1)S(1)} custom-call(bf16[1664,128]{1,0:T(8,128)(2,1)S(1)} %copy-done.1, bf16[2048,768]{1,0:T(8,128)(2,1)S(1)} %bitcast.22, f32[1152,128]{1,0:T(8,128)S(1)} %bitcast.26, bf16[1024,128]{1,0:T(8,128)(2,1)S(1)} %get-tuple-element.17.hot_ref, bf16[1024,128]{1,0:T(8,128)(2,1)S(1)} %get-tuple-element.18.mask_ref, ...), custom_call_target="tpu_custom_call" | custom-call | tf_op jit(solution)/shard_map/sums/pallas_call | solution.py:28
  125.1 56.5 %all_to_all.36 = bf16[16,104,128]{2,1,0:T(8,128)(2,1)S(1)} all-to-all(bf16[16,104,128]{2,1,0:T(8,128)(2,1)S(1)} %bitcast.33), channel_id=1, replica_groups=mesh['row'=64,'col'=16] {'col'}, dimensions={0} | all-to-all | bytes 851968 | tf_op jit(solution)/shard_map/all_to_all | solution.py:413
  181.7 0.3 update.2
  182.0 17.9 %all_to_all.37 = bf16[16,104,128]{2,1,0:T(8,128)(2,1)S(1)} all-to-all(bf16[16,104,128]{2,1,0:T(8,128)(2,1)S(1)} %bitcast.38), channel_id=1, replica_groups=mesh['row'=64,'col'=16] {'col'}, dimensions={0} | all-to-all | bytes 851968 | tf_op jit(solution)/shard_map/all_to_all | solution.py:424
  199.8 1.2 stats.3
  201.1 23.5 %all_to_all.38 = f32[64,8,2,128]{3,2,1,0:T(2,128)S(1)} all-to-all(f32[64,8,2,128]{3,2,1,0:T(2,128)S(1)} %bitcast.31), channel_id=1, replica_groups=mesh['row'=64,'col'=16] {'row'}, dimensions={0} | all-to-all | bytes 1048576 | tf_op jit(solution)/shard_map/all_to_all | solution.py:395
  224.6 3.3 %sums.3 = bf16[1664,128]{1,0:T(8,128)(2,1)S(1)} custom-call(bf16[1664,128]{1,0:T(8,128)(2,1)S(1)} %bitcast.28, bf16[2048,768]{1,0:T(8,128)(2,1)S(1)} %bitcast.24, f32[1024,128]{1,0:T(8,128)S(1)} %bitcast.30, bf16[1024,128]{1,0:T(8,128)(2,1)S(1)} %get-tuple-element.17.hot_ref, bf16[1024,128]{1,0:T(8,128)(2,1)S(1)} %get-tuple-element.18.mask_ref, ...), custom_call_target="tpu_custom_call" | custom-call | tf_op jit(solution)/shard_map/sums/pallas_call | solution.py:28
  228.0 19.4 %all_to_all.39 = bf16[16,104,128]{2,1,0:T(8,128)(2,1)S(1)} all-to-all(bf16[16,104,128]{2,1,0:T(8,128)(2,1)S(1)} %bitcast.32), channel_id=1, replica_groups=mesh['row'=64,'col'=16] {'col'}, dimensions={0} | all-to-all | bytes 851968 | tf_op jit(solution)/shard_map/all_to_all | solution.py:413
  247.4 0.7 update.3
  248.1 17.9 %all_to_all.40 = bf16[16,104,128]{2,1,0:T(8,128)(2,1)S(1)} all-to-all(bf16[16,104,128]{2,1,0:T(8,128)(2,1)S(1)} %bitcast.39), channel_id=1, replica_groups=mesh['row'=64,'col'=16] {'col'}, dimensions={0} | all-to-all | bytes 851968 | tf_op jit(solution)/shard_map/all_to_all | solution.py:424
  266.0 1.1 finish.1
  (5 shorter events, 0.0 us)
Async XLA Ops:
  5.1 14.1 %copy-start.4 = (f32[1,256]{1,0:T(1,128)S(1)}, f32[1,256]{1,0:T(1,128)}, u32[]{:S(2)}) copy-start(f32[1,256]{1,0:T(1,128)} %param.7) | copy-start | bytes 3076
  5.1 14.2 %copy-start.3 = (s32[1,32,4]{1,2,0:T(4,128)S(1)}, s32[1,32,4]{1,2,0:T(4,128)}, u32[]{:S(2)}) copy-start(s32[1,32,4]{1,2,0:T(4,128)} %param.5) | copy-start | bytes 1540
  5.1 82.5 %all-to-all-start = ((bf16[64,32,768]{2,1,0:T(8,128)(2,1)}), bf16[64,32,768]{2,1,0:T(8,128)(2,1)S(1)}, u32[]{:S(2)}, u32[]{:S(2)}) async-start(bf16[64,32,768]{2,1,0:T(8,128)(2,1)} %bitcast.42), calls=%async_computation | async-start | bytes 6291456 | tf_op jit(solution)/shard_map/all_to_all | solution.py:367
  19.3 1.1 copy-start.2
  20.7 0.8 copy-start
  87.5 1.0 copy-start.1
